TPU v7x, 32 devices: a 4x4x1 block of a 4x4x8 slice. The times are simulated.
32 devices in a mesh: dp: 1 (over z), tp: 32 (over y, x, core).
Axes of the slice: x: 4, y: 4, z: 1, core: 2. Of those that a mesh axis runs over, the one named last changes fastest.
The devices are a block of a 4x4x8 slice.
Arguments:
- ids: int32 [2, 256], P('dp')
- emb: bfloat16 [65536, 3584], P('tp')
- g: bfloat16 [3584], replicated
- w: bfloat16 [3584, 8192], P(None, 'tp')
- du: bfloat16 [2, 256, 8192], P('dp', None, 'tp')
- dres: bfloat16 [2, 256, 3584], P('dp', 'tp')
Outputs:
- output 1: bfloat16 [2, 256, 8192], P('dp', None, 'tp')
- output 2: bfloat16 [2, 256, 3584], P('dp', 'tp')
- output 3: float32 [65536, 3584], P(('dp', 'tp'))
- output 4: float32 [3584, 8192], P(None, ('dp', 'tp'))
- output 5: float32 [3584], P('dp')
All inputs are finite; a program needn't handle non-finite values.
Results may differ from a plain program's by a relative error of at most 0.001.
Values are sent between devices in bfloat16 or wider.
A program may use at most 768 MiB of HBM per device.

v0:
```python
import jax
import jax.numpy as jnp
from jax import lax
from jax.sharding import PartitionSpec as P

EPS = 1e-6


def solution(mesh):
    groups = mesh.shape["tp"]

    def local(ids, emb, g, w, du, dres):
        r = lax.axis_index("tp")
        t = ids.shape[1]
        vl, d = emb.shape
        tl = t // groups
        lo = r * vl
        start = r * tl
        gf = g.astype(jnp.float32)
        cols = lax.broadcasted_iota(jnp.int32, (1, vl), 1)

        def micro(dg, inp):
            idm, dum, drm = inp
            oh = ((idm - lo)[:, None] == cols).astype(jnp.bfloat16)
            xp = jnp.dot(oh, emb, preferred_element_type=jnp.float32).astype(jnp.bfloat16)
            x = lax.psum(xp, "tp")
            xf = x.astype(jnp.float32)
            rs = lax.rsqrt(jnp.mean(xf * xf, axis=-1, keepdims=True) + EPS)
            nh = xf * rs
            n = (nh * gf).astype(jnp.bfloat16)
            u = jnp.dot(n, w, preferred_element_type=jnp.float32).astype(jnp.bfloat16)
            pdn = jnp.einsum("tf,df->td", dum, w, preferred_element_type=jnp.float32).astype(jnp.bfloat16)
            recv = lax.all_to_all(pdn, "tp", 0, 0, tiled=True).reshape(groups, tl, d)
            dn = jnp.sum(recv.astype(jnp.float32), axis=0)
            nhs = lax.dynamic_slice_in_dim(nh, start, tl, 0)
            rss = lax.dynamic_slice_in_dim(rs, start, tl, 0)
            gdn = gf * dn
            dxn = rss * (gdn - nhs * jnp.mean(nhs * gdn, axis=-1, keepdims=True))
            dx = (drm.astype(jnp.float32) + dxn).astype(jnp.bfloat16)
            dxa = lax.all_gather(dx, "tp", axis=0, tiled=True)
            dg = dg + jnp.sum(dn * nhs, axis=0)
            return dg, (u, lax.dynamic_slice_in_dim(x, start, tl, 0), n, dxa)

        dg, (u, xo, ns, dxs) = lax.scan(micro, jnp.zeros((d,), jnp.float32), (ids, du, dres))
        loc = (ids - lo).reshape(-1)
        oh = (lax.broadcasted_iota(jnp.int32, (vl, loc.shape[0]), 0) == loc[None, :]).astype(jnp.bfloat16)
        de = jnp.dot(oh, dxs.reshape(-1, d), preferred_element_type=jnp.float32)
        dw = jnp.einsum("ktd,ktf->df", ns, du, preferred_element_type=jnp.float32)
        dg = lax.psum(dg, "tp")
        return u, xo, de, dw, dg

    return jax.shard_map(
        local,
        mesh=mesh,
        in_specs=(P("dp", None), P("tp", None), P(None), P(None, "tp"), P("dp", None, "tp"), P("dp", "tp", None)),
        out_specs=(P("dp", None, "tp"), P("dp", "tp", None), P(("dp", "tp"), None), P(None, ("dp", "tp")), P("dp")),
        check_vma=False,
    )
```

profile of v0, /device:TPU:97, one launch (start us, length us, event | category | flops | bytes accessed | tf_op | source)
XLA Modules:
  0.0 422.9 jit_solution(427461498960453525)
XLA Ops:
  7.2 0.7 subtract_bitcast_fusion
  7.9 0.7 convert_element_type.48
  8.6 343.8 %while.21 = (s32[]{:T(128)}, f32[3584]{0:T(1024)S(1)}, bf16[2,256,256]{2,1,0:T(8,128)(2,1)S(1)}, bf16[2,8,3584]{2,1,0:T(8,128)(2,1)S(1)}, bf16[2,256,3584]{2,1,0...) while((s32[]{:T(128)}, f32[3584]{0:T(1024)S(1)}, ...), condition=%wide.region_6.7_spmd.clone, body=%wide.region_0.6_spmd.clone.sunk | while | flops 4715044864 | bytes 109303496 | solution.py:44
  8.6 0.1 all-reduce.2.cloned.1.call-start
  8.6 0.7 fusion.34
  9.3 10.6 %convolution_convert_fusion.4 = bf16[256,3584]{1,0:T(8,128)(2,1)} fusion(bf16[2048,3584]{1,0:T(8,128)(2,1)} %get-tuple-element.395, s32[256]{0:T(256)S(1)} %bitcast.53), kind=kOutput, calls=%fused_computation.1.clone.1 | convolution fusion | flops 3759538176 | bytes 16516096 | tf_op jit(solution)/shard_map/while/body/eval_jaxpr/dot_general | solution.py:25
  19.9 0.1 all-reduce.2.cloned.1.call-update
  20.0 0.0 copy-done.1
  20.0 0.0 copy-done.2
  20.0 2.0 fusion.33
  22.0 9.1 %all-to-all-start = ((bf16[32,8,3584]{2,1,0:T(8,128)(2,1)}), bf16[32,8,3584]{2,1,0:T(8,128)(2,1)}, u32[]{:S(2)}, u32[]{:S(2)}) async-start(bf16[32,8,3584]{2,1,0:T(8,128)(2,1)} %fusion.33), calls=%async_computation | async-start | bytes 3670016 | tf_op jit(solution)/shard_map/while/body/eval_jaxpr/all_to_all | solution.py:33
  31.2 0.1 all-gather.2.cloned.1.call-start
  31.2 101.0 %all-reduce.2.cloned.1.call-done = bf16[256,3584]{1,0:T(8,128)(2,1)} async-done(((bf16[256,3584]{1,0:T(8,128)(2,1)}), bf16[256,3584]{1,0:T(8,128)(2,1)}) %all-reduce.2.cloned.1.call-update) | async-done | bytes 1835024 | tf_op jit(solution)/shard_map/while/body/eval_jaxpr/psum | solution.py:26
  132.2 1.9 fusion.35
  134.2 0.1 dynamic-slice.5
  134.2 3.9 convert_multiply_fusion.4
  138.2 0.0 all-to-all-done
  138.2 1.8 convert_reduce_fusion.2
  139.9 1.1 multiply_reduce_fusion.3
  141.0 0.0 copy-done.3
  141.0 1.6 fusion.37
  142.6 0.1 all-gather.2.cloned.1.call-update
  142.7 0.0 copy-start.5
  142.7 0.0 copy-done
  142.7 2.4 fusion.36
  145.1 0.2 copy-done.5
  145.3 0.6 bitcast_dynamic-update-slice_fusion.7
  145.9 0.0 copy-start.6
  145.9 1.8 copy-done.6
  147.8 32.9 %all-gather.2.cloned.1.call-done = bf16[256,3584]{1,0:T(8,128)(2,1)} async-done(((bf16[8,3584]{1,0:T(8,128)(2,1)}), bf16[256,3584]{1,0:T(8,128)(2,1)}) %all-gather.2.cloned.1.call-update) | async-done | bytes 1835024 | tf_op jit(solution)/shard_map/while/body/eval_jaxpr/all_gather | solution.py:40
  180.7 2.9 bitcast_dynamic-update-slice_fusion.8
  183.6 0.0 all-reduce.2.cloned.1.call-start
  183.6 0.7 fusion.34
  184.3 10.6 %convolution_convert_fusion.4 = bf16[256,3584]{1,0:T(8,128)(2,1)} fusion(bf16[2048,3584]{1,0:T(8,128)(2,1)} %get-tuple-element.395, s32[256]{0:T(256)S(1)} %bitcast.53), kind=kOutput, calls=%fused_computation.1.clone.1 | convolution fusion | flops 3759538176 | bytes 16516096 | tf_op jit(solution)/shard_map/while/body/eval_jaxpr/dot_general | solution.py:25
  194.9 0.1 all-reduce.2.cloned.1.call-update
  194.9 0.0 copy-done.1
  194.9 0.0 copy-done.2
  194.9 2.0 fusion.33
  196.9 4.1 all-to-all-start
  201.0 0.1 all-gather.2.cloned.1.call-start
  201.1 100.0 %all-reduce.2.cloned.1.call-done = bf16[256,3584]{1,0:T(8,128)(2,1)} async-done(((bf16[256,3584]{1,0:T(8,128)(2,1)}), bf16[256,3584]{1,0:T(8,128)(2,1)}) %all-reduce.2.cloned.1.call-update) | async-done | bytes 1835024 | tf_op jit(solution)/shard_map/while/body/eval_jaxpr/psum | solution.py:26
  301.0 1.9 fusion.35
  303.0 0.1 dynamic-slice.5
  303.1 3.9 convert_multiply_fusion.4
  307.0 0.0 all-to-all-done
  307.0 1.8 convert_reduce_fusion.2
  308.8 1.1 multiply_reduce_fusion.3
  309.8 0.0 copy-done.3
  309.8 1.6 fusion.37
  311.5 0.1 all-gather.2.cloned.1.call-update
  311.5 0.0 copy-start.5
  311.5 0.0 copy-done
  311.6 2.4 fusion.36
  313.9 0.2 copy-done.5
  314.1 0.6 bitcast_dynamic-update-slice_fusion.7
  314.8 0.0 copy-start.6
  314.8 1.8 copy-done.6
  316.6 32.9 %all-gather.2.cloned.1.call-done = bf16[256,3584]{1,0:T(8,128)(2,1)} async-done(((bf16[8,3584]{1,0:T(8,128)(2,1)}), bf16[256,3584]{1,0:T(8,128)(2,1)}) %all-gather.2.cloned.1.call-update) | async-done | bytes 1835024 | tf_op jit(solution)/shard_map/while/body/eval_jaxpr/all_gather | solution.py:40
  349.5 2.8 bitcast_dynamic-update-slice_fusion.8
  352.4 44.5 %psum.16 = f32[3584]{0:T(1024)} all-reduce(f32[3584]{0:T(1024)S(1)} %get-tuple-element.186), channel_id=1, replica_groups=mesh['dp'=1,'tp'=32] {'tp'}, use_global_device_ids=true, to_apply=%region_7.8 | all-reduce | flops 3584 | bytes 28672 | tf_op jit(solution)/shard_map/psum | solution.py:49
  396.9 5.2 %convolution_bitcast_fusion = f32[3584,256]{1,0:T(8,128)} fusion(bf16[2,256,3584]{2,1,0:T(8,128)(2,1)} %get-tuple-element.185, bf16[2,256,256]{2,1,0:T(8,128)(2,1)} %get-tuple-element.409), kind=kOutput, calls=%fused_computation.29 | convolution fusion | flops 939524096 | bytes 7602176 | tf_op jit(solution)/shard_map/ktd,ktf->df/dot_general | solution.py:48
  402.1 0.0 copy-done.7
  402.1 0.0 copy-done.8
  402.1 14.3 %fusion.12 = f32[2048,3584]{1,0:T(8,128)} fusion(bf16[512,3584]{1,0:T(8,128)(2,1)S(1)} %bitcast.55, s32[512]{0:T(512)S(1)} %bitcast.54), kind=kOutput, calls=%fused_computation.31 | convolution fusion | flops 7517241344 | bytes 33032192 | tf_op jit(solution)/shard_map/dot_general | solution.py:47
  (26 shorter events, 0.1 us)
Async XLA Ops:
  8.6 123.6 %all-reduce.2.cloned.1.call-start = ((), (), s32[]{:S(2)}) async-start(), calls=%async_computation.1 | async-start | bytes 3670016 | tf_op jit(solution)/shard_map/while/body/eval_jaxpr/psum | solution.py:26
  9.3 10.6 %copy-start.1 = (bf16[3584,256]{1,0:T(8,128)(2,1)S(1)}, bf16[3584,256]{1,0:T(8,128)(2,1)}, u32[]{:S(2)}) copy-start(bf16[3584,256]{1,0:T(8,128)(2,1)} %get-tuple-element.392) | copy-start | bytes 5505028 | tf_op jit(solution)/shard_map/while
  9.3 10.7 %copy-start.2 = (bf16[2,256,256]{2,1,0:T(8,128)(2,1)S(1)}, bf16[2,256,256]{2,1,0:T(8,128)(2,1)}, u32[]{:S(2)}) copy-start(bf16[2,256,256]{2,1,0:T(8,128)(2,1)} %get-tuple-element.391) | copy-start | bytes 786436 | tf_op jit(solution)/shard_map/while
  22.0 116.2 %all-to-all-start = ((bf16[32,8,3584]{2,1,0:T(8,128)(2,1)}), bf16[32,8,3584]{2,1,0:T(8,128)(2,1)}, u32[]{:S(2)}, u32[]{:S(2)}) async-start(bf16[32,8,3584]{2,1,0:T(8,128)(2,1)} %fusion.33), calls=%async_computation | async-start | bytes 3670016 | tf_op jit(solution)/shard_map/while/body/eval_jaxpr/all_to_all | solution.py:33
  31.2 149.6 %all-gather.2.cloned.1.call-start = ((), (), s32[]{:S(2)}) async-start(), calls=%async_computation.2 | async-start | bytes 1892352 | tf_op jit(solution)/shard_map/while/body/eval_jaxpr/all_gather | solution.py:40
  134.2 6.8 %copy-start.3 = (bf16[2,8,3584]{2,1,0:T(8,128)(2,1)S(1)}, bf16[2,8,3584]{2,1,0:T(8,128)(2,1)}, u32[]{:S(2)}) copy-start(bf16[2,8,3584]{2,1,0:T(8,128)(2,1)} %get-tuple-element.398) | copy-start | bytes 344068 | tf_op jit(solution)/shard_map/while
  134.2 8.5 %copy-start = (bf16[256,3584]{1,0:T(8,128)(2,1)S(1)}, bf16[256,3584]{1,0:T(8,128)(2,1)}, u32[]{:S(2)}) copy-start(bf16[256,3584]{1,0:T(8,128)(2,1)} %all-reduce.2.cloned.1.call-done) | copy-start | bytes 5505028 | tf_op jit(solution)/shard_map/while
  142.7 2.6 copy-start.5
  145.9 1.8 copy-start.6
  183.6 117.4 %all-reduce.2.cloned.1.call-start = ((), (), s32[]{:S(2)}) async-start(), calls=%async_computation.1 | async-start | bytes 3670016 | tf_op jit(solution)/shard_map/while/body/eval_jaxpr/psum | solution.py:26
  184.3 10.6 %copy-start.1 = (bf16[3584,256]{1,0:T(8,128)(2,1)S(1)}, bf16[3584,256]{1,0:T(8,128)(2,1)}, u32[]{:S(2)}) copy-start(bf16[3584,256]{1,0:T(8,128)(2,1)} %get-tuple-element.392) | copy-start | bytes 5505028 | tf_op jit(solution)/shard_map/while
  184.3 10.7 %copy-start.2 = (bf16[2,256,256]{2,1,0:T(8,128)(2,1)S(1)}, bf16[2,256,256]{2,1,0:T(8,128)(2,1)}, u32[]{:S(2)}) copy-start(bf16[2,256,256]{2,1,0:T(8,128)(2,1)} %get-tuple-element.391) | copy-start | bytes 786436 | tf_op jit(solution)/shard_map/while
  196.9 110.1 %all-to-all-start = ((bf16[32,8,3584]{2,1,0:T(8,128)(2,1)}), bf16[32,8,3584]{2,1,0:T(8,128)(2,1)}, u32[]{:S(2)}, u32[]{:S(2)}) async-start(bf16[32,8,3584]{2,1,0:T(8,128)(2,1)} %fusion.33), calls=%async_computation | async-start | bytes 3670016 | tf_op jit(solution)/shard_map/while/body/eval_jaxpr/all_to_all | solution.py:33
  201.0 148.5 %all-gather.2.cloned.1.call-start = ((), (), s32[]{:S(2)}) async-start(), calls=%async_computation.2 | async-start | bytes 1892352 | tf_op jit(solution)/shard_map/while/body/eval_jaxpr/all_gather | solution.py:40
  303.1 6.8 %copy-start.3 = (bf16[2,8,3584]{2,1,0:T(8,128)(2,1)S(1)}, bf16[2,8,3584]{2,1,0:T(8,128)(2,1)}, u32[]{:S(2)}) copy-start(bf16[2,8,3584]{2,1,0:T(8,128)(2,1)} %get-tuple-element.398) | copy-start | bytes 344068 | tf_op jit(solution)/shard_map/while
  303.1 8.5 %copy-start = (bf16[256,3584]{1,0:T(8,128)(2,1)S(1)}, bf16[256,3584]{1,0:T(8,128)(2,1)}, u32[]{:S(2)}) copy-start(bf16[256,3584]{1,0:T(8,128)(2,1)} %all-reduce.2.cloned.1.call-done) | copy-start | bytes 5505028 | tf_op jit(solution)/shard_map/while
  311.5 2.6 copy-start.5
  314.8 1.8 copy-start.6
  352.4 49.7 %copy-start.7 = (bf16[2,8,3584]{2,1,0:T(8,128)(2,1)}, bf16[2,8,3584]{2,1,0:T(8,128)(2,1)S(1)}, u32[]{:S(2)}) copy-start(bf16[2,8,3584]{2,1,0:T(8,128)(2,1)S(1)} %get-tuple-element.178) | copy-start | bytes 344068
  352.4 49.7 %copy-start.8 = (bf16[2,256,256]{2,1,0:T(8,128)(2,1)}, bf16[2,256,256]{2,1,0:T(8,128)(2,1)S(1)}, u32[]{:S(2)}) copy-start(bf16[2,256,256]{2,1,0:T(8,128)(2,1)S(1)} %get-tuple-element.177) | copy-start | bytes 786436
  396.9 5.2 %copy-start.4 = (bf16[2,256,3584]{2,1,0:T(8,128)(2,1)S(1)}, bf16[2,256,3584]{2,1,0:T(8,128)(2,1)}, u32[]{:S(2)}) copy-start(bf16[2,256,3584]{2,1,0:T(8,128)(2,1)} %get-tuple-element.184) | copy-start | bytes 11010052
Sparse Core Ops, SparseCore 0:
  20.1 112.0 all-reduce.1
  142.8 37.8 all-gather.1
  195.0 105.9 all-reduce.1
  311.6 37.8 all-gather.1
where the time goes:
time: 424 us; the launch traced here: 423 us
  waiting for transfers between devices  267 us (63%)
  matrix products  49.4 us (12%)
  blocking collectives  44.5 us (10%)
  other arithmetic  24.7 us (6%)
  between operations  13.7 us (3%)
  starting transfers between devices  13.4 us (3%)
  local copies, waits for them, and re-layouts  9.95 us (2%)
    psum x2, waiting for transfers between devices, micro(): x = lax.psum(xp, 'tp')  201 us
    all_gather x2, waiting for transfers between devices, micro(): dxa = lax.all_gather(dx, 'tp', axis=0, tiled=True)  65.8 us
    psum x1, blocking collectives, local(): dg = lax.psum(dg, 'tp')  44.5 us
    dot_general x2, matrix products, micro(): jnp.dot(oh, emb, preferred_element_type=jnp.float32).astype(jnp.bfloat16)  21.2 us
    dot_general x1, matrix products, local(): de = jnp.dot(oh, dxs.reshape(-1, d), preferred_element_type=jnp.float32)  14.3 us
    all_to_all x2, starting transfers between devices, micro(): recv = lax.all_to_all(pdn, 'tp', 0, 0, tiled=True).reshape(groups, tl, d)  13.2 us
  transfers between devices with their start and end apart: 6, of which 4 were waited for; matrix products, arithmetic and copies ran while one was open for 5% of the time, Pallas kernels for 0%

commit v1 on v0

v1 whole, which is shorter than its diff:
```python
import functools
import math

import jax
import jax.numpy as jnp
from jax import lax
from jax.experimental import pallas as pl
from jax.experimental.pallas import tpu as pltpu
from jax.sharding import PartitionSpec as P

EPS = 1e-6
F32 = jnp.float32
BF16 = jnp.bfloat16
VMEM = pltpu.VMEM
DMA = pltpu.SemaphoreType.DMA


def comm_kernel(dims, loc_ref, emb_ref, g_ref, w_ref, du_ref, dres_ref,
                x_ref, nall_ref, dxall_ref, dg_ref,
                ebuf, esem, dup, oh, pdn, rpdn, s1, r1, t1, r2, xp, rxp, rx1, tx, rx2,
                own, gn, gd, dgp, dgs, dgx, dgy,
                pair_s, pair_r, rs_s, rs_r, ag_s, ag_r, sib_s, sib_r, dg_s, dg_r, osem):
    k, tl, d, n = dims["k"], dims["tl"], dims["d"], dims["n"]
    dh, dq, cw = d // 2, d // 4, dims["cw"]
    nch = dh // cw
    tb = k * tl
    me = lax.axis_index("tp")
    c = lax.rem(me, 2)
    x = lax.rem(me // 2, n)
    y = me // (2 * n)

    def dev(yy, xx, cc):
        return {"tp": (yy * n + xx) * 2 + cc}

    def add(v, s):
        return lax.rem(v + s + n, n)

    coord = {"x": x, "y": y}

    def peer(axis, s):
        return dev(y, add(x, s), c) if axis == "x" else dev(add(y, s), x, c)

    sib = dev(y, x, 1 - c)
    sends = []

    def remote(src, dst, ss, rs, to):
        cp = pltpu.make_async_remote_copy(src_ref=src, dst_ref=dst, send_sem=ss, recv_sem=rs,
                                          device_id=to, device_id_type=pl.DeviceIdType.MESH)
        cp.start()
        sends.append(cp)
        return cp

    barrier = pltpu.get_barrier_semaphore()
    greet = [sib] + [peer(a, s) for a in ("x", "y") for s in (1, -1, 2)]
    for to in greet:
        pl.semaphore_signal(barrier, inc=1, device_id=to, device_id_type=pl.DeviceIdType.MESH)

    eload = []
    for h in range(2):
        cp = pltpu.make_async_copy(emb_ref.at[:, pl.ds(h * dh, dh)], ebuf.at[h], esem.at[h])
        cp.start()
        eload.append(cp)

    duf = [du_ref[m].astype(F32) for m in range(k)]
    for cc in range(2):
        for b in range(n * n):
            r = b * 2 + cc
            blk = jnp.concatenate([v[r * tl:(r + 1) * tl] for v in duf], axis=0)
            dup[pl.ds((cc * n * n + b) * tb, tb), :] = blk.astype(BF16)

    def scatter_rows(dst, h, j, val):
        cols = pl.ds(pl.multiple_of(j * cw, cw), cw)
        for cc in range(2):
            for yy in range(n):
                for xx in range(n):
                    p, q = (xx, yy) if h == 0 else (yy, xx)
                    row = ((cc * n + yy) * n + xx) * tb
                    dst[h, cc, p, pl.ds(q * tb, tb), cols] = val[row:row + tb]

    pair = []
    for h in range(2):
        @pl.loop(0, nch)
        def _(j):
            wj = w_ref[pl.ds(pl.multiple_of(h * dh + j * cw, cw), cw), :]
            v = lax.dot_general(dup[...], wj, (((1,), (1,)), ((), ())), preferred_element_type=F32)
            scatter_rows(pdn, h, j, v.astype(BF16))

        if h == 0:
            pl.semaphore_wait(barrier, len(greet))
        pair.append(remote(pdn.at[h, 1 - c], rpdn.at[h], pair_s.at[0, h], pair_r.at[0, h], sib))

    ids = lax.broadcasted_iota(jnp.int32, (tb * n, oh.shape[1]), 1)
    for i in range(2 * n):
        rows = pl.ds(i * tb * n, tb * n)
        oh[rows, :] = (loc_ref[rows, :] == ids).astype(BF16)

    class Ring:
        def __init__(self, sem, axis, s, r):
            self.sem, self.axis, self.s, self.r = sem, axis, s, r
            self.p = coord[axis]

        def half(self, sgn):
            return pl.ds(0 if sgn > 0 else dq, dq)

        def send(self, msg, sgn, block, half):
            i = 0 if sgn > 0 else 1
            st, h, ph = self.sem
            return remote(self.s.at[block, :, half], self.r.at[msg, i],
                          rs_s.at[st, h, ph, msg, i], rs_r.at[st, h, ph, msg, i], peer(self.axis, sgn))

        def start(self):
            self.a1 = [self.send(0, sg, add(self.p, 2), self.half(sg)) for sg in (1, -1)]
            self.a2 = [self.send(1, sg, add(self.p, sg), self.half(-sg)) for sg in (1, -1)]

        def mid(self):
            self.b = []
            for i, sg in enumerate((1, -1)):
                self.a1[i].wait_recv()
                blk, hf = add(self.p, sg), self.half(sg)
                self.s[blk, :, hf] = self.s[blk, :, hf] + self.r[0, i]
                self.b.append(self.send(2, sg, blk, hf))

        def finish(self):
            for cp in self.a2 + self.b:
                cp.wait_recv()
            for i, sg in enumerate((1, -1)):
                hf = self.half(sg)
                yield hf, self.s[self.p, :, hf] + self.r[2, i] + self.r[1, 1 - i]

    axes = [("x", "y"), ("y", "x")]

    def first(st, h, s, r):
        return Ring((st, h, 0), axes[h][0], s, r.at[h])

    def second(st, h, t, r):
        return Ring((st, h, 1), axes[h][1], t.at[h], r.at[h])

    d1 = [first(0, h, s1.at[h], r1) for h in range(2)]
    d2 = [second(0, h, t1, r2) for h in range(2)]
    x1 = [first(1, h, xp.at[h, c], rx1) for h in range(2)]
    x2 = [second(1, h, tx, rx2) for h in range(2)]

    def finish1(ring, t, h):
        for hf, v in ring.finish():
            t[h, :, :, hf] = v.reshape(n, tb, dq)

    for h in range(2):
        pair[h].wait_recv()
        for p in range(n):
            s1[h, p] = pdn[h, c, p].astype(F32) + rpdn[h, p].astype(F32)
        d1[h].start()

    xpair = []
    for h in range(2):
        eload[h].wait()

        @pl.loop(0, nch)
        def _(j):
            ej = ebuf[h, :, pl.ds(pl.multiple_of(j * cw, cw), cw)]
            v = jnp.dot(oh[...], ej, preferred_element_type=F32)
            scatter_rows(xp, h, j, v.astype(BF16))

        xpair.append(remote(xp.at[h, 1 - c], rxp.at[h], pair_s.at[1, h], pair_r.at[1, h], sib))
        if h == 0:
            for hh in range(2):
                d1[hh].mid()

    for h in range(2):
        xpair[h].wait_recv()
        for p in range(n):
            xp[h, c, p] = xp[h, c, p] + rxp[h, p]
        x1[h].start()
    for h in range(2):
        finish1(d1[h], t1, h)
        d2[h].start()
    for h in range(2):
        x1[h].mid()
    for h in range(2):
        d2[h].mid()
    for h in range(2):
        finish1(x1[h], tx, h)
        x2[h].start()
    for h in range(2):
        x2[h].mid()

    class Gather:
        def __init__(self, sem, axis, get):
            self.sem, self.axis, self.get = sem, axis, get
            self.p = coord[axis]

        def send(self, msg, sgn, block, half):
            i = 0 if sgn > 0 else 1
            st, h, ph = self.sem
            ref = self.get(block, half)
            return remote(ref, ref, ag_s.at[st, h, ph, msg, i], ag_r.at[st, h, ph, msg, i],
                          peer(self.axis, sgn))

        def start(self):
            self.a = [self.send(0, sg, self.p, pl.ds(0, dh)) for sg in (1, -1)]

        def mid(self):
            self.b = []
            for i, sg in enumerate((1, -1)):
                self.a[i].wait_recv()
                self.b.append(self.send(1, sg, add(self.p, -sg), pl.ds(0 if sg > 0 else dq, dq)))

        def finish(self):
            for cp in self.b:
                cp.wait_recv()

    def gathers(st, g):
        ph1, ph2 = [], []
        ph1.append(Gather((st, 0, 0), "x", lambda i, hf: g.at[0, c, y, i, :, hf]))
        ph2.append(Gather((st, 0, 1), "y", lambda i, hf: g.at[0, c, i, :, :, hf]))
        ph1.append(Gather((st, 1, 0), "y", lambda i, hf: g.at[1, c, i, x, :, hf]))
        ph2.append(Gather((st, 1, 1), "x", lambda i, hf: g.at[1, c, :, i, :, hf]))
        return ph1, ph2

    n1, n2 = gathers(0, gn)
    e1, e2 = gathers(1, gd)

    for h in range(2):
        for hf, v in x2[h].finish():
            own[0, h, :, hf] = v.astype(F32)
    ss = jnp.zeros((tb, 1), F32)
    for h in range(2):
        v = own[0, h]
        ss = ss + jnp.sum(v * v, axis=-1, keepdims=True)
    rs = lax.rsqrt(ss / d + EPS)
    for h in range(2):
        gf = g_ref[:, pl.ds(h * dh, dh)].astype(F32)
        gn[h, c, y, x] = (own[0, h] * rs * gf).astype(BF16)
        n1[h].start()
    for h in range(2):
        v = own[0, h]
        for m in range(k):
            x_ref[m, :, pl.ds(h * dh, dh)] = v[m * tl:(m + 1) * tl].astype(BF16)

    for h in range(2):
        for hf, v in d2[h].finish():
            own[1, h, :, hf] = v
    dot = jnp.zeros((tb, 1), F32)
    for h in range(2):
        gf = g_ref[:, pl.ds(h * dh, dh)].astype(F32)
        nh = own[0, h] * rs
        dot = dot + jnp.sum(nh * (gf * own[1, h]), axis=-1, keepdims=True)
    dot = dot / d
    for h in range(2):
        gf = g_ref[:, pl.ds(h * dh, dh)].astype(F32)
        nh = own[0, h] * rs
        dxn = rs * (gf * own[1, h] - nh * dot)
        dr = jnp.concatenate([dres_ref[m, :, pl.ds(h * dh, dh)].astype(F32) for m in range(k)], axis=0)
        gd[h, c, y, x] = (dr + dxn).astype(BF16)
        e1[h].start()
    for h in range(2):
        dgp[:, pl.ds(h * dh, dh)] = jnp.sum(own[1, h] * (own[0, h] * rs), axis=0, keepdims=True)
    dgpair = remote(dgp, dgs, dg_s.at[0], dg_r.at[0], sib)

    for h in range(2):
        n1[h].mid()
    for h in range(2):
        e1[h].mid()

    def spread(buf, axis, base):
        return [remote(buf.at[coord[axis]], buf.at[coord[axis]], dg_s.at[base + i], dg_r.at[base + i],
                       peer(axis, s)) for i, s in enumerate((1, -1, 2))]

    def total(buf):
        v = buf[0]
        for i in range(1, n):
            v = v + buf[i]
        return v

    dgpair.wait_recv()
    dgx[x] = dgp[...] + dgs[...]
    sx = spread(dgx, "x", 1)
    for h in range(2):
        n1[h].finish()
        n2[h].start()
    for h in range(2):
        e1[h].finish()
        e2[h].start()
    for cp in sx:
        cp.wait_recv()
    dgy[y] = total(dgx)
    sy = spread(dgy, "y", 4)
    for h in range(2):
        n2[h].mid()
    for h in range(2):
        e2[h].mid()

    outs = []

    def put(st, g, out, cc, i):
        cp = pltpu.make_async_copy(g.at[:, cc], out.at[:, cc], osem.at[st, i])
        cp.start()
        outs.append(cp)

    def to_sib(st, g):
        return [remote(g.at[h, c], g.at[h, c], sib_s.at[st, h], sib_r.at[st, h], sib) for h in range(2)]

    for h in range(2):
        n2[h].finish()
    bn = to_sib(0, gn)
    put(0, gn, nall_ref, c, 0)
    for cp in sy:
        cp.wait_recv()
    dg_ref[...] = total(dgy)
    for h in range(2):
        e2[h].finish()
    bd = to_sib(1, gd)
    put(1, gd, dxall_ref, c, 0)
    for cp in bn:
        cp.wait_recv()
    put(0, gn, nall_ref, 1 - c, 1)
    for cp in bd:
        cp.wait_recv()
    put(1, gd, dxall_ref, 1 - c, 1)
    for cp in sends:
        cp.wait_send()
    for cp in outs:
        cp.wait()


def tail_kernel(dims, loc_ref, n_ref, dx_ref, w_ref, du_ref, u_ref, de_ref, dw_ref, oh, dup, uacc):
    k, tl, side = dims["k"], dims["tl"], dims["n"]
    tb = k * tl
    j = pl.program_id(0)
    step = min(256, oh.shape[0])

    @pl.when(j == 0)
    def _():
        @pl.loop(0, oh.shape[0] // step)
        def _(i):
            ids = lax.broadcasted_iota(jnp.int32, (step, oh.shape[1]), 0) + i * step
            oh[pl.ds(pl.multiple_of(i * step, step), step), :] = (ids == loc_ref[...]).astype(BF16)

        duf = [du_ref[m].astype(F32) for m in range(k)]
        for cc in range(2):
            for b in range(side * side):
                r = b * 2 + cc
                blk = jnp.concatenate([v[r * tl:(r + 1) * tl] for v in duf], axis=0)
                dup[pl.ds((cc * side * side + b) * tb, tb), :] = blk.astype(BF16)
        uacc[...] = jnp.zeros_like(uacc)

    nv = n_ref[0]
    de_ref[...] = jnp.dot(oh[...], dx_ref[0], preferred_element_type=F32)
    dw_ref[...] = lax.dot_general(nv, dup[...], (((0,), (0,)), ((), ())), preferred_element_type=F32)
    uacc[...] += jnp.dot(nv, w_ref[...], preferred_element_type=F32)

    @pl.when(j == pl.num_programs(0) - 1)
    def _():
        for m in range(k):
            parts = []
            for b in range(side * side):
                for cc in range(2):
                    row = (cc * side * side + b) * tb + m * tl
                    parts.append(uacc[pl.ds(row, tl), :])
            u_ref[m] = jnp.concatenate(parts, axis=0).astype(BF16)


def solution(mesh):
    groups = mesh.shape["tp"]
    side = math.isqrt(groups // 2)

    def local(ids, emb, g, w, du, dres):
        r = lax.axis_index("tp")
        k, t = ids.shape
        vl, d = emb.shape
        f = w.shape[1]
        tl = t // groups
        tb = k * tl
        n = side
        dh, dq = d // 2, d // 4
        cw = 256 if dh % 256 == 0 else 128
        nch = dh // cw
        dims = dict(k=k, tl=tl, d=d, n=n, cw=cw)
        loc = ids.reshape(k, n, n, 2, tl).transpose(3, 1, 2, 0, 4).reshape(-1) - r * vl
        hbm = pl.BlockSpec(memory_space=pl.ANY)
        vm = pl.BlockSpec(memory_space=pltpu.VMEM)
        gshape = (2, 2, n, n, tb, dh)
        xo, nall, dxall, dg = pl.pallas_call(
            functools.partial(comm_kernel, dims),
            out_shape=[
                jax.ShapeDtypeStruct((k, tl, d), BF16),
                jax.ShapeDtypeStruct(gshape, BF16),
                jax.ShapeDtypeStruct(gshape, BF16),
                jax.ShapeDtypeStruct((1, d), F32),
            ],
            in_specs=[vm, hbm, vm, vm, vm, vm],
            out_specs=[vm, hbm, hbm, vm],
            scratch_shapes=[
                VMEM((2, vl, dh), BF16), DMA((2,)),
                VMEM((k * t, f), BF16), VMEM((k * t, vl), BF16),
                VMEM((2, 2, n, n * tb, dh), BF16), VMEM((2, n, n * tb, dh), BF16),
                VMEM((2, n, n * tb, dh), F32), VMEM((2, 3, 2, n * tb, dq), F32),
                VMEM((2, n, tb, dh), F32), VMEM((2, 3, 2, tb, dq), F32),
                VMEM((2, 2, n, n * tb, dh), BF16), VMEM((2, n, n * tb, dh), BF16),
                VMEM((2, 3, 2, n * tb, dq), BF16),
                VMEM((2, n, tb, dh), BF16), VMEM((2, 3, 2, tb, dq), BF16),
                VMEM((2, 2, tb, dh), F32), VMEM(gshape, BF16), VMEM(gshape, BF16),
                VMEM((1, d), F32), VMEM((1, d), F32), VMEM((n, 1, d), F32), VMEM((n, 1, d), F32),
                DMA((2, 2)), DMA((2, 2)),
                DMA((2, 2, 2, 3, 2)), DMA((2, 2, 2, 3, 2)),
                DMA((2, 2, 2, 2, 2)), DMA((2, 2, 2, 2, 2)),
                DMA((2, 2)), DMA((2, 2)),
                DMA((7,)), DMA((7,)), DMA((2, 2)),
            ],
            compiler_params=pltpu.CompilerParams(collective_id=0, has_side_effects=True,
                                                 vmem_limit_bytes=62 * 1024 * 1024),
        )(loc[:, None], emb, g[None, :], w, du, dres)
        u, de, dw = pl.pallas_call(
            functools.partial(tail_kernel, dims),
            grid=(2 * nch,),
            out_shape=[
                jax.ShapeDtypeStruct((k, t, f), BF16),
                jax.ShapeDtypeStruct((vl, d), F32),
                jax.ShapeDtypeStruct((d, f), F32),
            ],
            in_specs=[
                pl.BlockSpec((1, k * t), lambda j: (0, 0)),
                pl.BlockSpec((1, k * t, cw), lambda j: (j // nch, 0, j % nch)),
                pl.BlockSpec((1, k * t, cw), lambda j: (j // nch, 0, j % nch)),
                pl.BlockSpec((cw, f), lambda j: (j, 0)),
                pl.BlockSpec((k, t, f), lambda j: (0, 0, 0)),
            ],
            out_specs=[
                pl.BlockSpec((k, t, f), lambda j: (0, 0, 0)),
                pl.BlockSpec((vl, cw), lambda j: (0, j)),
                pl.BlockSpec((cw, f), lambda j: (j, 0)),
            ],
            scratch_shapes=[VMEM((vl, k * t), BF16), VMEM((k * t, f), BF16), VMEM((k * t, f), F32)],
        )(loc[None, :], nall.reshape(2, k * t, dh), dxall.reshape(2, k * t, dh), w, du)
        return u, xo, de, dw, dg.reshape(d)

    return jax.shard_map(
        local,
        mesh=mesh,
        in_specs=(P("dp", None), P("tp", None), P(None), P(None, "tp"), P("dp", None, "tp"), P("dp", "tp", None)),
        out_specs=(P("dp", None, "tp"), P("dp", "tp", None), P(("dp", "tp"), None), P(None, ("dp", "tp")), P("dp")),
        check_vma=False,
    )
```

time: 424 us -> 106 us (0.25)
  waiting for transfers between devices: 267 us -> 0 us
  Pallas kernels: 0 us -> 100 us
  matrix products: 49.4 us -> 0 us
  blocking collectives: 44.5 us -> 0 us
  other arithmetic: 24.7 us -> 1.33 us
  starting transfers between devices: 13.4 us -> 0 us
  between operations: 13.7 us -> 0.66 us
  local copies, waits for them, and re-layouts: 9.95 us -> 3.63 us
    psum x2 -> x0, waiting for transfers between devices: 201 us -> none  [micro(): x = lax.psum(xp, 'tp')]
    pallas_call x0 -> x2, Pallas kernels: none -> 100 us  [the longest x1 79.5 us: local(): pl.pallas_call(functools.partial(comm_kernel, dims), out_shape=[jax.Shape...]
    all_gather x2 -> x0, waiting for transfers between devices: 65.8 us -> none  [micro(): dxa = lax.all_gather(dx, 'tp', axis=0, tiled=True)]
    dot_general x8 -> x0, matrix products: 49.4 us -> none  [the longest x2 21.2 us: micro(): jnp.dot(oh, emb, preferred_element_type=jnp.float32).astype(jnp.bfloat16)]
    psum x1 -> x0, blocking collectives: 44.5 us -> none  [local(): dg = lax.psum(dg, 'tp')]
    all_to_all x2 -> x0, starting transfers between devices: 13.2 us -> none  [micro(): recv = lax.all_to_all(pdn, 'tp', 0, 0, tiled=True).reshape(groups, tl, d)]
    reduce_sum x6 -> x0, other arithmetic: 9.53 us -> none  [the longest x2 3.88 us: micro(): rs = lax.rsqrt(jnp.mean(xf * xf, axis=-1, keepdims=True) + EPS)]
    mul x2 -> x0, other arithmetic: 7.89 us -> none  [micro(): nh = xf * rs]
  transfers between devices with their start and end apart: 6 -> 0, of which waited for: 4 -> 0; matrix products, arithmetic and copies ran while one was open for 5% -> 0% of each run, Pallas kernels for 0% -> 0%
where the time goes in v1:
time: 106 us
  Pallas kernels  100 us (94%)
  local copies, waits for them, and re-layouts  3.63 us (3%)
  other arithmetic  1.33 us (1%)
    pallas_call x1, Pallas kernels, local(): pl.pallas_call(functools.partial(comm_kernel, dims), out_shape=[jax.Shape...  79.5 us
    pallas_call x1, Pallas kernels, local(): pl.pallas_call(functools.partial(tail_kernel, dims), grid=(2 * nch,), out...  20.6 us

profile of v1, /device:TPU:97, one launch (start us, length us, event | category | flops | bytes accessed | tf_op | source)
XLA Modules:
  0.0 105.7 jit_solution(18133298277980537721)
XLA Ops:
  0.6 0.7 broadcast_subtract_fusion
  1.3 0.1 sub.36
  1.5 0.9 sub.40.loc_ref
  2.3 1.3 %broadcast_in_dim.2.g_ref = bf16[1,3584]{1,0:T(2,128)(2,1)} reshape(bf16[3584]{0:T(1024)(128)(2,1)} %param.8) | data formatting | bytes 14336 | tf_op jit(solution)/shard_map/broadcast_in_dim | solution.py:411
  3.6 79.5 %shard_map.101 = (bf16[2,8,3584]{2,1,0:T(8,128)(2,1)}, bf16[2,2,4,4,16,1792]{5,4,3,2,1,0:T(8,128)(2,1)}, bf16[2,2,4,4,16,1792]{5,4,3,2,1,0:T(8,128)(2,1)}, f32[1,3584]{1,0:T(1,128)}) custom-call(s32[512,1]{1,0:T(8,128)} %sub.40.loc_ref, bf16[2048,3584]{1,0:T(8,128)(2,1)} %emb_ref.1, bf16[1,3584]{1,0:T(2,128)(2,1)} %broadcast_in_dim.2.g_ref, ...), custom_call_target="tpu_custom_call" | custom-call | tf_op jit(solution)/shard_map/pallas_call | solution.py:382
  83.1 0.7 sub.38.loc_ref
  83.8 0.0 copy-start.1
  83.8 0.0 copy-start
  83.8 20.6 %shard_map.102 = (bf16[2,256,256]{2,1,0:T(8,128)(2,1)}, f32[2048,3584]{1,0:T(8,128)}, f32[3584,256]{1,0:T(8,128)}) custom-call(s32[1,512]{1,0:T(1,128)} %sub.38.loc_ref, bf16[2,512,1792]{2,1,0:T(8,128)(2,1)} %bitcast.5, bf16[2,512,1792]{2,1,0:T(8,128)(2,1)} %bitcast.6, bf16[3584,256]{1,0:T(8,128)(2,1)} %w_ref.3, bf16[2,256,256]{2,1,0:T(8,128)(2,1)} %du_ref.3), custom_call_target="tpu_custom_call" | custom-call | tf_op jit(solution)/shard_map/pallas_call | solution.py:412
  104.4 0.0 copy-done.1
  104.4 0.6 reduce
  105.1 0.0 copy-done
  105.1 0.6 copy.17
  (1 shorter events, 0.0 us)
Async XLA Ops:
  83.8 20.6 %copy-start.1 = (f32[1,3584]{1,0:T(1,128)S(1)}, f32[1,3584]{1,0:T(1,128)}, u32[]{:S(2)}) copy-start(f32[1,3584]{1,0:T(1,128)} %get-tuple-element.18) | copy-start | bytes 43012
  83.8 21.2 %copy-start = (bf16[2,8,3584]{2,1,0:T(8,128)(2,1)S(1)}, bf16[2,8,3584]{2,1,0:T(8,128)(2,1)}, u32[]{:S(2)}) copy-start(bf16[2,8,3584]{2,1,0:T(8,128)(2,1)} %get-tuple-element.25) | copy-start | bytes 344068

commit v2 on v1

v2 whole, which is shorter than its diff:
```python
import functools
import math

import jax
import jax.numpy as jnp
from jax import lax
from jax.experimental import pallas as pl
from jax.experimental.pallas import tpu as pltpu
from jax.sharding import PartitionSpec as P

EPS = 1e-6
F32 = jnp.float32
BF16 = jnp.bfloat16
VMEM = pltpu.VMEM
DMA = pltpu.SemaphoreType.DMA


def comm_kernel(dims, ids_ref, emb_ref, g_ref, w_ref, du_ref, dres_ref,
                x_ref, nall_ref, dxall_ref, dg_ref, tab_ref,
                ebuf, esem, oh, pdn, rpdn, s1, r1, t1, r2, xp, rxp, rx1, tx, rx2,
                own, gn, gd, dgp, dgs, dgx, dgy,
                pair_s, pair_r, rs_s, rs_r, ag_s, ag_r, sib_s, sib_r, dg_s, dg_r, osem):
    k, tl, d, n = dims["k"], dims["tl"], dims["d"], dims["n"]
    dh, dq, cw = d // 2, d // 4, dims["cw"]
    nch = dh // cw
    tb = k * tl
    t = du_ref.shape[1]
    vl = emb_ref.shape[0]
    me = lax.axis_index("tp")
    c = lax.rem(me, 2)
    x = lax.rem(me // 2, n)
    y = me // (2 * n)

    def dev(yy, xx, cc):
        return {"tp": (yy * n + xx) * 2 + cc}

    def add(v, s):
        return lax.rem(v + s + n, n)

    coord = {"x": x, "y": y}

    def peer(axis, s):
        return dev(y, add(x, s), c) if axis == "x" else dev(add(y, s), x, c)

    gall = g_ref[...].astype(F32).reshape(1, d)
    sib = dev(y, x, 1 - c)
    sends = []

    def remote(src, dst, ss, rs, to):
        cp = pltpu.make_async_remote_copy(src_ref=src, dst_ref=dst, send_sem=ss, recv_sem=rs,
                                          device_id=to, device_id_type=pl.DeviceIdType.MESH)
        cp.start()
        sends.append(cp)
        return cp

    barrier = pltpu.get_barrier_semaphore()
    greet = [sib] + [peer(a, s) for a in ("x", "y") for s in (1, -1, 2)]
    for to in greet:
        pl.semaphore_signal(barrier, inc=1, device_id=to, device_id_type=pl.DeviceIdType.MESH)

    eload = []
    for h in range(2):
        cp = pltpu.make_async_copy(emb_ref.at[:, pl.ds(h * dh, dh)], ebuf.at[h], esem.at[h])
        cp.start()
        eload.append(cp)

    def scatter_rows(dst, h, j, val):
        cols = pl.ds(pl.multiple_of(j * cw, cw), cw)
        for cc in range(2):
            for yy in range(n):
                for xx in range(n):
                    p, q = (xx, yy) if h == 0 else (yy, xx)
                    row = ((yy * n + xx) * 2 + cc) * tl
                    blk = jnp.concatenate([val[m * t + row:m * t + row + tl] for m in range(k)], axis=0)
                    dst[h, cc, p, pl.ds(q * tb, tb), cols] = blk.astype(BF16)

    for h in range(2):
        @pl.loop(0, nch)
        def _(j):
            wj = w_ref[pl.ds(pl.multiple_of(h * dh + j * cw, cw), cw), :]
            v = lax.dot_general(du_ref[...].reshape(k * t, -1), wj,
                                (((1,), (1,)), ((), ())), preferred_element_type=F32)
            scatter_rows(pdn, h, j, v)

    pl.semaphore_wait(barrier, len(greet))
    pair = [remote(pdn.at[h, 1 - c], rpdn.at[h], pair_s.at[0, h], pair_r.at[0, h], sib) for h in range(2)]

    loc = ids_ref[...] - me * vl
    locp = jnp.concatenate([loc, jnp.zeros((8 - k, t), jnp.int32)], axis=0) if k < 8 else loc
    loct = jnp.transpose(locp)
    step = 64
    ids = lax.broadcasted_iota(jnp.int32, (step, vl), 1)
    for m in range(k):
        for i in range(t // step):
            rows = pl.ds(m * t + i * step, step)
            oh[rows, :] = (loct[i * step:(i + 1) * step, m:m + 1] == ids).astype(BF16)

    nt = k * t
    keyc = jnp.concatenate([loct[:, m:m + 1] for m in range(k)], axis=0)
    keyr = jnp.concatenate([loc[m:m + 1] for m in range(k)], axis=1)
    posc = lax.broadcasted_iota(jnp.int32, (nt, 1), 0)
    posr = lax.broadcasted_iota(jnp.int32, (1, nt), 1)
    okr = (keyr >= 0) & (keyr < vl)
    okc = (keyc >= 0) & (keyc < vl)
    sortr = jnp.where(okr, keyr, vl) * nt + posr
    sortc = jnp.where(okc, keyc, vl) * nt + posc
    rank = jnp.sum((sortr < sortc).astype(F32), axis=1, keepdims=True)
    hit = rank == posr.astype(F32)
    tok = posc % t
    blk = tok // tl
    place = ((blk % 2) * n * n + blk // 2) * tb + (posc // t) * tl + tok % tl
    tab_ref[0:1, :] = jnp.sum(jnp.where(hit, keyc.astype(F32), 0.0), axis=0, keepdims=True).astype(jnp.int32)
    tab_ref[1:2, :] = jnp.sum(jnp.where(hit, place.astype(F32), 0.0), axis=0, keepdims=True).astype(jnp.int32)
    below = okc & (keyc < posr * dims["rt"])
    tab_ref[2:3, :] = jnp.sum(below.astype(F32), axis=0, keepdims=True).astype(jnp.int32)

    class Ring:
        def __init__(self, sem, axis, s, r):
            self.sem, self.axis, self.s, self.r = sem, axis, s, r
            self.p = coord[axis]

        def half(self, sgn):
            return pl.ds(0 if sgn > 0 else dq, dq)

        def send(self, msg, sgn, block, half):
            i = 0 if sgn > 0 else 1
            st, h, ph = self.sem
            return remote(self.s.at[block, :, half], self.r.at[msg, i],
                          rs_s.at[st, h, ph, msg, i], rs_r.at[st, h, ph, msg, i], peer(self.axis, sgn))

        def start(self):
            self.a1 = [self.send(0, sg, add(self.p, 2), self.half(sg)) for sg in (1, -1)]
            self.a2 = [self.send(1, sg, add(self.p, sg), self.half(-sg)) for sg in (1, -1)]

        def mid(self):
            self.b = []
            for i, sg in enumerate((1, -1)):
                self.a1[i].wait_recv()
                blk, hf = add(self.p, sg), self.half(sg)
                self.s[blk, :, hf] = self.s[blk, :, hf] + self.r[0, i]
                self.b.append(self.send(2, sg, blk, hf))

        def finish(self):
            for cp in self.a2 + self.b:
                cp.wait_recv()
            for i, sg in enumerate((1, -1)):
                hf = self.half(sg)
                yield hf, self.s[self.p, :, hf] + self.r[2, i] + self.r[1, 1 - i]

    axes = [("x", "y"), ("y", "x")]

    def first(st, h, s, r):
        return Ring((st, h, 0), axes[h][0], s, r.at[h])

    def second(st, h, t, r):
        return Ring((st, h, 1), axes[h][1], t.at[h], r.at[h])

    d1 = [first(0, h, s1.at[h], r1) for h in range(2)]
    d2 = [second(0, h, t1, r2) for h in range(2)]
    x1 = [first(1, h, xp.at[h, c], rx1) for h in range(2)]
    x2 = [second(1, h, tx, rx2) for h in range(2)]

    def finish1(ring, t, h):
        for hf, v in ring.finish():
            t[h, :, :, hf] = v.reshape(n, tb, dq)

    def emm(h, lo, hi):
        @pl.loop(lo, hi)
        def _(j):
            ej = ebuf[h, :, pl.ds(pl.multiple_of(j * cw, cw), cw)]
            v = jnp.dot(oh[...], ej, preferred_element_type=F32)
            scatter_rows(xp, h, j, v)

    def start_d1(h):
        pair[h].wait_recv()
        for p in range(n):
            s1[h, p] = pdn[h, c, p].astype(F32) + rpdn[h, p].astype(F32)
        d1[h].start()

    def send_x(h):
        return remote(xp.at[h, 1 - c], rxp.at[h], pair_s.at[1, h], pair_r.at[1, h], sib)

    def start_x1(h):
        xpair[h].wait_recv()
        for p in range(n):
            xp[h, c, p] = xp[h, c, p] + rxp[h, p]
        x1[h].start()

    cuts = [nch // 7, 2 * nch // 7, 3 * nch // 7]
    eload[0].wait()
    emm(0, 0, cuts[0])
    start_d1(0)
    emm(0, cuts[0], cuts[1])
    start_d1(1)
    emm(0, cuts[1], nch)
    xpair = [send_x(0)]
    eload[1].wait()
    emm(1, 0, cuts[2])
    start_x1(0)
    emm(1, cuts[2], nch)
    xpair.append(send_x(1))
    for h in range(2):
        d1[h].mid()
    start_x1(1)
    for h in range(2):
        x1[h].mid()
    finish1(x1[0], tx, 0)
    x2[0].start()
    finish1(d1[0], t1, 0)
    d2[0].start()
    finish1(x1[1], tx, 1)
    x2[1].start()
    finish1(d1[1], t1, 1)
    d2[1].start()
    for h in range(2):
        x2[h].mid()
    for h in range(2):
        d2[h].mid()

    outs = []

    class Gather:
        def __init__(self, sem, axis, get, put=None):
            self.sem, self.axis, self.get, self.put = sem, axis, get, put
            self.p = coord[axis]
            self.sibs = []

        def send(self, msg, sgn, block, half):
            i = 0 if sgn > 0 else 1
            st, h, ph = self.sem
            ref = self.get(c, block, half)
            return remote(ref, ref, ag_s.at[st, h, ph, msg, i], ag_r.at[st, h, ph, msg, i],
                          peer(self.axis, sgn))

        def have(self, s):
            if self.put is None:
                return
            st, h, _ = self.sem
            i = s % n
            ref = self.get(c, add(self.p, s), pl.ds(0, dh))
            self.sibs.append((s, remote(ref, ref, sib_s.at[st, h, i], sib_r.at[st, h, i], sib)))
            self.out(c, s, 0)

        def out(self, cc, s, side):
            st, h, _ = self.sem
            block = add(self.p, s)
            cp = pltpu.make_async_copy(self.get(cc, block, pl.ds(0, dh)), self.put(cc, block),
                                       osem.at[st, h, side, s % n])
            cp.start()
            outs.append(cp)

        def start(self):
            self.a = [self.send(0, sg, self.p, pl.ds(0, dh)) for sg in (1, -1)]
            self.have(0)

        def mid(self):
            self.b = []
            for i, sg in enumerate((1, -1)):
                self.a[i].wait_recv()
                self.b.append(self.send(1, sg, add(self.p, -sg), pl.ds(0 if sg > 0 else dq, dq)))
                self.have(-sg)

        def finish(self):
            for cp in self.b:
                cp.wait_recv()
            self.have(2)

        def drain(self, count):
            for s, cp in self.sibs[:count]:
                cp.wait_recv()
                self.out(1 - c, s, 1)
            self.sibs = self.sibs[count:]

    def gathers(st, g, out):
        ph1, ph2 = [], []
        c0, c1 = pl.ds(0, dh), pl.ds(dh, dh)
        ph1.append(Gather((st, 0, 0), "x", lambda cc, i, hf: g.at[0, cc, y, i, :, hf]))
        ph2.append(Gather((st, 0, 1), "y", lambda cc, i, hf: g.at[0, cc, i, :, :, hf],
                          lambda cc, i: out.at[cc, i, :, :, c0]))
        ph1.append(Gather((st, 1, 0), "y", lambda cc, i, hf: g.at[1, cc, i, x, :, hf]))
        ph2.append(Gather((st, 1, 1), "x", lambda cc, i, hf: g.at[1, cc, :, i, :, hf],
                          lambda cc, i: out.at[cc, :, i, :, c1]))
        return ph1, ph2

    n1, n2 = gathers(0, gn, nall_ref)
    e1, e2 = gathers(1, gd, dxall_ref)

    for h in range(2):
        for hf, v in x2[h].finish():
            own[0, h, :, hf] = v.astype(F32)
    ss = jnp.zeros((tb, 1), F32)
    for h in range(2):
        v = own[0, h]
        ss = ss + jnp.sum(v * v, axis=-1, keepdims=True)
    rs = lax.rsqrt(ss / d + EPS)
    for h in range(2):
        gf = gall[:, h * dh:(h + 1) * dh]
        gn[h, c, y, x] = (own[0, h] * rs * gf).astype(BF16)
        n1[h].start()
    for h in range(2):
        v = own[0, h]
        for m in range(k):
            x_ref[m, :, pl.ds(h * dh, dh)] = v[m * tl:(m + 1) * tl].astype(BF16)

    for h in range(2):
        for hf, v in d2[h].finish():
            own[1, h, :, hf] = v
    dot = jnp.zeros((tb, 1), F32)
    for h in range(2):
        gf = gall[:, h * dh:(h + 1) * dh]
        nh = own[0, h] * rs
        dot = dot + jnp.sum(nh * (gf * own[1, h]), axis=-1, keepdims=True)
    dot = dot / d
    for h in range(2):
        gf = gall[:, h * dh:(h + 1) * dh]
        nh = own[0, h] * rs
        dxn = rs * (gf * own[1, h] - nh * dot)
        dr = jnp.concatenate([dres_ref[m, :, pl.ds(h * dh, dh)].astype(F32) for m in range(k)], axis=0)
        gd[h, c, y, x] = (dr + dxn).astype(BF16)
        e1[h].start()
    for h in range(2):
        dgp[:, pl.ds(h * dh, dh)] = jnp.sum(own[1, h] * (own[0, h] * rs), axis=0, keepdims=True)
    dgpair = remote(dgp, dgs, dg_s.at[0], dg_r.at[0], sib)

    for h in range(2):
        n1[h].mid()
    for h in range(2):
        e1[h].mid()

    def spread(buf, axis, base):
        return [remote(buf.at[coord[axis]], buf.at[coord[axis]], dg_s.at[base + i], dg_r.at[base + i],
                       peer(axis, s)) for i, s in enumerate((1, -1, 2))]

    def total(buf):
        v = buf[0]
        for i in range(1, n):
            v = v + buf[i]
        return v

    dgpair.wait_recv()
    dgx[x] = dgp[...] + dgs[...]
    sx = spread(dgx, "x", 1)
    for h in range(2):
        n1[h].finish()
        n2[h].start()
    for h in range(2):
        e1[h].finish()
        e2[h].start()
    for cp in sx:
        cp.wait_recv()
    dgy[y] = total(dgx)
    sy = spread(dgy, "y", 4)
    for h in range(2):
        n2[h].mid()
    for h in range(2):
        e2[h].mid()

    for h in range(2):
        n2[h].finish()
    for cp in sy:
        cp.wait_recv()
    dg_ref[...] = total(dgy).reshape(d)
    for h in range(2):
        n2[h].drain(4)
    for h in range(2):
        e2[h].drain(1)
    for h in range(2):
        e2[h].finish()
    for i in (2, 1):
        for h in range(2):
            e2[h].drain(i)
    for cp in sends:
        cp.wait_send()
    for cp in outs:
        cp.wait()


def tail_kernel(dims, tab_ref, n_ref, dx_ref, w_ref, du_ref, x_ref, dg_ref,
                u_ref, de_ref, dw_ref, xo_ref, dgo_ref, dxf, dup, uacc):
    k, tl, side = dims["k"], dims["tl"], dims["n"]
    tb = k * tl
    rt = dims["rt"]
    j = pl.program_id(0)

    @pl.when(j == 0)
    def _():
        dxf[...] = dx_ref[...].astype(F32)

    de_ref[...] = jnp.zeros_like(de_ref)

    @pl.loop(tab_ref[2, j], tab_ref[2, j + 1])
    def _(i):
        row = pl.ds(tab_ref[0, i] - j * rt, 1)
        de_ref[row, :] = de_ref[row, :] + dxf[pl.ds(tab_ref[1, i], 1), :]

    @pl.when(j == 0)
    def _():
        duf = [du_ref[m].astype(F32) for m in range(k)]
        for cc in range(2):
            for b in range(side * side):
                r = b * 2 + cc
                blk = jnp.concatenate([v[r * tl:(r + 1) * tl] for v in duf], axis=0)
                dup[pl.ds((cc * side * side + b) * tb, tb), :] = blk.astype(BF16)
        uacc[...] = jnp.zeros_like(uacc)
        xo_ref[...] = x_ref[...]
        dgo_ref[...] = dg_ref[...]

    @pl.when((j > 0) & (j <= dims["nw"]))
    def _():
        nv = n_ref[...]
        dw_ref[...] = lax.dot_general(nv, dup[...], (((0,), (0,)), ((), ())), preferred_element_type=F32)
        uacc[...] += jnp.dot(nv, w_ref[...], preferred_element_type=F32)

    @pl.when(j == pl.num_programs(0) - 1)
    def _():
        for m in range(k):
            parts = []
            for b in range(side * side):
                for cc in range(2):
                    row = (cc * side * side + b) * tb + m * tl
                    parts.append(uacc[pl.ds(row, tl), :])
            u_ref[m] = jnp.concatenate(parts, axis=0).astype(BF16)


def solution(mesh):
    groups = mesh.shape["tp"]
    side = math.isqrt(groups // 2)

    def local(ids, emb, g, w, du, dres):
        k, t = ids.shape
        vl, d = emb.shape
        f = w.shape[1]
        tl = t // groups
        tb = k * tl
        n = side
        dh, dq = d // 2, d // 4
        cw = 256 if dh % 256 == 0 else 128
        rt = vl // 8
        wc = d // 7 if d % 896 == 0 else d // 4
        nw = d // wc
        dims = dict(k=k, tl=tl, d=d, n=n, cw=cw, rt=rt, nw=nw)
        hbm = pl.BlockSpec(memory_space=pl.ANY)
        vm = pl.BlockSpec(memory_space=pltpu.VMEM)
        gshape = (2, 2, n, n, tb, dh)
        oshape = (2, n, n, tb, d)
        xo, nall, dxall, dg, tab = pl.pallas_call(
            functools.partial(comm_kernel, dims),
            out_shape=[
                jax.ShapeDtypeStruct((k, tl, d), BF16),
                jax.ShapeDtypeStruct(oshape, BF16),
                jax.ShapeDtypeStruct(oshape, BF16),
                jax.ShapeDtypeStruct((d,), F32),
                jax.ShapeDtypeStruct((8, k * t), jnp.int32),
            ],
            in_specs=[vm, hbm, vm, vm, vm, vm],
            out_specs=[vm, hbm, hbm, vm, vm],
            scratch_shapes=[
                VMEM((2, vl, dh), BF16), DMA((2,)),
                VMEM((k * t, vl), BF16),
                VMEM((2, 2, n, n * tb, dh), BF16), VMEM((2, n, n * tb, dh), BF16),
                VMEM((2, n, n * tb, dh), F32), VMEM((2, 3, 2, n * tb, dq), F32),
                VMEM((2, n, tb, dh), F32), VMEM((2, 3, 2, tb, dq), F32),
                VMEM((2, 2, n, n * tb, dh), BF16), VMEM((2, n, n * tb, dh), BF16),
                VMEM((2, 3, 2, n * tb, dq), BF16),
                VMEM((2, n, tb, dh), BF16), VMEM((2, 3, 2, tb, dq), BF16),
                VMEM((2, 2, tb, dh), F32), VMEM(gshape, BF16), VMEM(gshape, BF16),
                VMEM((1, d), F32), VMEM((1, d), F32), VMEM((n, 1, d), F32), VMEM((n, 1, d), F32),
                DMA((2, 2)), DMA((2, 2)),
                DMA((2, 2, 2, 3, 2)), DMA((2, 2, 2, 3, 2)),
                DMA((2, 2, 2, 2, 2)), DMA((2, 2, 2, 2, 2)),
                DMA((2, 2, n)), DMA((2, 2, n)),
                DMA((7,)), DMA((7,)), DMA((2, 2, 2, n)),
            ],
            compiler_params=pltpu.CompilerParams(collective_id=0, has_side_effects=True,
                                                 vmem_limit_bytes=62 * 1024 * 1024),
        )(ids, emb, g, w, du, dres)
        u, de, dw, xo, dg = pl.pallas_call(
            functools.partial(tail_kernel, dims),
            grid=(vl // rt,),
            out_shape=[
                jax.ShapeDtypeStruct((k, t, f), BF16),
                jax.ShapeDtypeStruct((vl, d), F32),
                jax.ShapeDtypeStruct((d, f), F32),
                jax.ShapeDtypeStruct((k, tl, d), BF16),
                jax.ShapeDtypeStruct((d,), F32),
            ],
            in_specs=[
                pl.BlockSpec(memory_space=pltpu.SMEM),
                pl.BlockSpec((k * t, wc), lambda j: (0, jnp.clip(j - 1, 0, nw - 1))),
                pl.BlockSpec((k * t, d), lambda j: (0, 0), pipeline_mode=pl.Buffered(1)),
                pl.BlockSpec((wc, f), lambda j: (jnp.clip(j - 1, 0, nw - 1), 0)),
                pl.BlockSpec((k, t, f), lambda j: (0, 0, 0)),
                pl.BlockSpec((k, tl, d), lambda j: (0, 0, 0)),
                pl.BlockSpec((d,), lambda j: (0,)),
            ],
            out_specs=[
                pl.BlockSpec((k, t, f), lambda j: (0, 0, 0)),
                pl.BlockSpec((rt, d), lambda j: (j, 0)),
                pl.BlockSpec((wc, f), lambda j: (jnp.clip(j - 1, 0, nw - 1), 0)),
                pl.BlockSpec((k, tl, d), lambda j: (0, 0, 0)),
                pl.BlockSpec((d,), lambda j: (0,)),
            ],
            scratch_shapes=[VMEM((k * t, d), F32), VMEM((k * t, f), BF16), VMEM((k * t, f), F32)],
            compiler_params=pltpu.CompilerParams(vmem_limit_bytes=62 * 1024 * 1024),
        )(tab, nall.reshape(k * t, d), dxall.reshape(k * t, d), w, du, xo, dg)
        return u, xo, de, dw, dg

    return jax.shard_map(
        local,
        mesh=mesh,
        in_specs=(P("dp", None), P("tp", None), P(None), P(None, "tp"), P("dp", None, "tp"), P("dp", "tp", None)),
        out_specs=(P("dp", None, "tp"), P("dp", "tp", None), P(("dp", "tp"), None), P(None, ("dp", "tp")), P("dp")),
        check_vma=False,
    )
```

time: 106 us -> 93.4 us (0.88)
  Pallas kernels: 100 us -> 92.5 us
  local copies, waits for them, and re-layouts: 3.63 us -> 0 us
  other arithmetic: 1.33 us -> 0 us
    pallas_call x1, Pallas kernels: 20.6 us -> 15.7 us  [local(): pl.pallas_call(functools.partial(tail_kernel, dims), grid=(vl // rt,), ou...]
    pallas_call x1, Pallas kernels: 79.5 us -> 76.8 us  [local(): pl.pallas_call(functools.partial(comm_kernel, dims), out_shape=[jax.Shape...]
    sub x4 -> x0, local copies, waits for them, and re-layouts: 1.67 us -> none  [local(): ids.reshape(k, n, n, 2, tl).transpose(3, 1, 2, 0, 4).reshape(-1) - r * vl]
    broadcast_in_dim x1 -> x0, local copies, waits for them, and re-layouts: 1.3 us -> none  [local(): g[None, :]]
where the time goes in v2:
time: 93.4 us; the launch traced here: 93.1 us
  Pallas kernels  92.5 us (99%)
    pallas_call x1, Pallas kernels, local(): pl.pallas_call(functools.partial(comm_kernel, dims), out_shape=[jax.Shape...  76.8 us
    pallas_call x1, Pallas kernels, local(): pl.pallas_call(functools.partial(tail_kernel, dims), grid=(vl // rt,), ou...  15.7 us

profile of v2, /device:TPU:97, one launch (start us, length us, event | category | flops | bytes accessed | tf_op | source)
XLA Modules:
  0.0 93.1 jit_solution(6731726939597722409)
XLA Ops:
  0.6 76.8 %shard_map.101 = (bf16[2,8,3584]{2,1,0:T(8,128)(2,1)}, bf16[2,4,4,16,3584]{4,3,2,1,0:T(8,128)(2,1)}, bf16[2,4,4,16,3584]{4,3,2,1,0:T(8,128)(2,1)}, f32[3584]{0:T(1024)}, s32[8,512]{1,0:T(8,128)}) custom-call(s32[2,256]{1,0:T(2,128)} %ids_ref.1, bf16[2048,3584]{1,0:T(8,128)(2,1)} %emb_ref.1, bf16[3584]{0:T(1024)(128)(2,1)} %g_ref.1, bf16[3584,256]{1,0:T(8,128)(2,1)} %w_ref.3, ...), custom_call_target="tpu_custom_call" | custom-call | tf_op jit(solution)/shard_map/pallas_call | solution.py:446
  77.4 15.7 %shard_map.102 = (bf16[2,256,256]{2,1,0:T(8,128)(2,1)}, f32[2048,3584]{1,0:T(8,128)}, f32[3584,256]{1,0:T(8,128)}, bf16[2,8,3584]{2,1,0:T(8,128)(2,1)}, f32[3584]{0:T(1024)}) custom-call(s32[8,512]{1,0:T(8,128)} %get-tuple-element.15.tab_ref, bf16[512,3584]{1,0:T(8,128)(2,1)} %bitcast.2, bf16[512,3584]{1,0:T(8,128)(2,1)} %bitcast.3, ...), custom_call_target="tpu_custom_call" | custom-call | tf_op jit(solution)/shard_map/pallas_call | solution.py:477

commit v3 on v2

v3 whole, which is shorter than its diff:
```python
import functools
import math

import jax
import jax.numpy as jnp
from jax import lax
from jax.experimental import pallas as pl
from jax.experimental.pallas import tpu as pltpu
from jax.sharding import PartitionSpec as P

EPS = 1e-6
F32 = jnp.float32
BF16 = jnp.bfloat16
VMEM = pltpu.VMEM
DMA = pltpu.SemaphoreType.DMA
BOTH = range(2)
WAYS = (1, -1)
SHIFTS = (2, 1, -1)
RING = {(0, 0): 0, (0, 1): 5, (1, 1): 8}


def comm_kernel(dims, ids_ref, emb_ref, g_ref, w_ref, du_ref, dres_ref,
                xout_ref, nall_ref, dxall_ref, dgout_ref, tabout_ref,
                ebuf, esem, oh, pdn, rpdn, s1, r1, t1, r2, xp, rxp, rx1, tx, rx2,
                own, gn, gd, dgp, dgs, dgx, dgy,
                pair_s, pair_r, rs_s, rs_r, ag_s, ag_r, sib_s, sib_r, dg_s, dg_r, osem,
                xc, rxc, rq, cc_e, fx, hop_s, hop_r, x_ref, dg_ref, tab_ref, small_sem):
    k, tl, d, n, fast = dims["k"], dims["tl"], dims["d"], dims["n"], dims["fast"]
    dh, dq, cw = d // 2, d // 4, dims["cw"]
    nch = dh // cw
    cb = dims["cb"]
    tb = k * tl
    t = du_ref.shape[1]
    vl = emb_ref.shape[0]
    me = lax.axis_index("tp")
    c = lax.rem(me, 2)
    x = lax.rem(me // 2, n)
    y = me // (2 * n)

    def dev(yy, xx, cc):
        return {"tp": (yy * n + xx) * 2 + cc}

    def add(v, s):
        return lax.rem(v + s + n, n)

    coord = {"x": x, "y": y}

    def peer(axis, s):
        return dev(y, add(x, s), c) if axis == "x" else dev(add(y, s), x, c)

    gall = g_ref[...].astype(F32).reshape(1, d)
    sib = dev(y, x, 1 - c)
    sends, outs = [], []

    def emit(i, src, dst):
        cp = pltpu.make_async_copy(src, dst, small_sem.at[i])
        cp.start()
        outs.append(cp)

    def remote(src, dst, ss, rs, to):
        cp = pltpu.make_async_remote_copy(src_ref=src, dst_ref=dst, send_sem=ss, recv_sem=rs,
                                          device_id=to, device_id_type=pl.DeviceIdType.MESH)
        cp.start()
        sends.append(cp)
        return cp

    barrier = pltpu.get_barrier_semaphore()
    greet = [sib] + [peer(a, s) for a in ("x", "y") for s in (1, -1, 2)]
    for to in greet:
        pl.semaphore_signal(barrier, inc=1, device_id=to, device_id_type=pl.DeviceIdType.MESH)

    eload = []
    for h in BOTH:
        cp = pltpu.make_async_copy(emb_ref.at[:, pl.ds(h * dh, dh)], ebuf.at[h], esem.at[h])
        cp.start()
        eload.append(cp)

    def scatter_rows(dst, h, j, val, cw):
        cols = pl.ds(pl.multiple_of(j * cw, cw), cw)
        for cc in BOTH:
            for yy in range(n):
                for xx in range(n):
                    p, q = (xx, yy) if h == 0 else (yy, xx)
                    row = ((yy * n + xx) * 2 + cc) * tl
                    blk = jnp.concatenate([val[m * t + row:m * t + row + tl] for m in range(k)], axis=0)
                    dst[h, cc, p, pl.ds(q * tb, tb), cols] = blk.astype(BF16)

    for h in BOTH:
        @pl.loop(0, dh // cb)
        def _(j):
            wj = w_ref[pl.ds(pl.multiple_of(h * dh + j * cb, cb), cb), :]
            v = lax.dot_general(du_ref[...].reshape(k * t, -1), wj,
                                (((1,), (1,)), ((), ())), preferred_element_type=F32)
            scatter_rows(pdn, h, j, v, cb)

    pl.semaphore_wait(barrier, len(greet))
    pair = [remote(pdn.at[h, 1 - c], rpdn.at[h], pair_s.at[0, h], pair_r.at[0, h], sib) for h in BOTH]

    loc = ids_ref[...] - me * vl
    locp = jnp.concatenate([loc, jnp.zeros((8 - k, t), jnp.int32)], axis=0) if k < 8 else loc
    loct = jnp.transpose(locp)
    if not fast:
        step = 64
        ids = lax.broadcasted_iota(jnp.int32, (step, vl), 1)
        for m in range(k):
            for i in range(t // step):
                rows = pl.ds(m * t + i * step, step)
                oh[rows, :] = (loct[i * step:(i + 1) * step, m:m + 1] == ids).astype(BF16)

    nt = k * t
    keyc = jnp.concatenate([loct[:, m:m + 1] for m in range(k)], axis=0)
    keyr = jnp.concatenate([loc[m:m + 1] for m in range(k)], axis=1)
    posc = lax.broadcasted_iota(jnp.int32, (nt, 1), 0)
    posr = lax.broadcasted_iota(jnp.int32, (1, nt), 1)

    class Facts:
        def __init__(self, key, pos):
            self.loc, self.pos = key, pos
            self.tok = pos % t
            blk = self.tok // tl
            self.c, self.at = blk % 2, {"x": (blk // 2) % n, "y": blk // (2 * n)}
            self.here = (key >= 0) & (key < vl)
            self.chip = (key + me * vl) // (2 * vl)
            self.owner = {"x": self.chip % n, "y": self.chip // n}

        def group(self, axis):
            return (self.at[axis] * 2 + self.c) * (n * n) + self.chip

    fr, fc = Facts(keyr, posr), Facts(keyc, posc)

    def rank_row(axis):
        m = (fc.group(axis) == fr.group(axis)) & (posc < posr)
        return jnp.sum(m.astype(F32), axis=0, keepdims=True).astype(jnp.int32)

    def rank_col(axis):
        m = (fc.group(axis) == fr.group(axis)) & (posr < posc)
        return jnp.sum(m.astype(F32), axis=1, keepdims=True).astype(jnp.int32)

    def pick(want, value):
        m = jnp.where(want, (value + 1).astype(F32), 0.0)
        return jnp.sum(m, axis=1, keepdims=True).astype(jnp.int32) - 1

    def table():
        sortr = jnp.where(fr.here, keyr, vl) * nt + posr
        sortc = jnp.where(fc.here, keyc, vl) * nt + posc
        rank = jnp.sum((sortr < sortc).astype(F32), axis=1, keepdims=True)
        hit = rank == posr.astype(F32)
        if fast:
            places = [(fc.c * n + fc.at["y"]) * tb + rank_col("y"), (fc.c * n + fc.at["x"]) * tb + rank_col("x")]
        else:
            place = ((fc.c * n + fc.at["y"]) * n + fc.at["x"]) * tb + (posc // t) * tl + fc.tok % tl
            places = [place]
        vals = [jnp.sum(jnp.where(hit, v.astype(F32), 0.0), axis=0, keepdims=True).astype(jnp.int32)
                for v in [keyc] + places]
        tab_ref[0:1, :] = vals[0]
        tab_ref[1:2, :] = vals[1]
        tab_ref[2:3, :] = vals[-1]
        below = fc.here & (keyc < posr * dims["rt"])
        tab_ref[3:4, :] = jnp.sum(below.astype(F32), axis=0, keepdims=True).astype(jnp.int32)
        tab_ref[4:, :] = jnp.full((4, nt), not fast, jnp.int32)
        emit(0, tab_ref, tabout_ref)

    if not fast:
        table()

    class Ring:
        def __init__(self, sem, axis, s, r, parts=1):
            self.sem, self.axis, self.s, self.r, self.parts = sem, axis, s, r, parts
            self.p = coord[axis]
            self.pr = s.shape[1] // parts
            self.b = []
            self.far_in = False

        def half(self, sgn):
            return pl.ds(0 if sgn > 0 else dq, dq)

        def rows(self, part):
            return pl.ds(part * self.pr, self.pr)

        def send(self, msg, sgn, block, half, part=None):
            i = 0 if sgn > 0 else 1
            st, h, ph = self.sem
            rows = slice(None) if part is None else self.rows(part)
            sem = (h, RING[st, ph] + msg + (part or 0) * 2, i) if fast else (st, h, ph, msg, i)
            return remote(self.s.at[block, rows, half], self.r.at[msg, i, rows],
                          rs_s.at[sem], rs_r.at[sem], peer(self.axis, sgn))

        def start(self):
            self.far()
            self.near(0)

        def far(self):
            self.a1 = [self.send(0, sg, add(self.p, 2), self.half(sg)) for sg in WAYS]

        def near(self, part):
            self.b += [self.send(1, sg, add(self.p, sg), self.half(-sg), part) for sg in WAYS]

        def mid(self, part=0):
            for i, sg in enumerate(WAYS):
                if not self.far_in:
                    self.a1[i].wait_recv()
                blk, rows, hf = add(self.p, sg), self.rows(part), self.half(sg)
                self.s[blk, rows, hf] = self.s[blk, rows, hf] + self.r[0, i, rows]
                self.b.append(self.send(2, sg, blk, hf, part))
            self.far_in = True

        def finish(self):
            for cp in self.b:
                cp.wait_recv()
            for i, sg in enumerate(WAYS):
                hf = self.half(sg)
                yield hf, self.s[self.p, :, hf] + self.r[2, i] + self.r[1, 1 - i]

    axes = [("x", "y"), ("y", "x")]

    def first(st, h, s, r):
        return Ring((st, h, 0), axes[h][0], s, r.at[h], 2 if fast and st == 0 else 1)

    def second(st, h, t, r):
        return Ring((st, h, 1), axes[h][1], t.at[h], r.at[h])

    d1 = [first(0, h, s1.at[h], r1) for h in BOTH]
    d2 = [second(0, h, t1, r2) for h in BOTH]
    x1 = [first(1, h, xp.at[h, c], rx1) for h in BOTH]
    x2 = [second(1, h, tx, rx2) for h in BOTH]

    def finish1(ring, t, h):
        for hf, v in ring.finish():
            t[h, :, :, hf] = v.reshape(n, tb, dq)

    def emm(h):
        @pl.loop(0, nch)
        def _(j):
            ej = ebuf[h, :, pl.ds(pl.multiple_of(j * cw, cw), cw)]
            v = jnp.dot(oh[...], ej, preferred_element_type=F32)
            scatter_rows(xp, h, j, v, cw)

    def start_d1(h):
        pair[h].wait_recv()
        for p in range(n):
            s1[h, p] = pdn[h, c, p].astype(F32) + rpdn[h, p].astype(F32)
        d1[h].far()
        if not fast:
            d1[h].near(0)

    def send_x(h):
        src, dst = (xc.at[h, 1 - c], rxc.at[h]) if fast else (xp.at[h, 1 - c], rxp.at[h])
        return remote(src, dst, pair_s.at[1, h], pair_r.at[1, h], sib)

    def start_x1(h):
        xpair[h].wait_recv()
        for p in range(n):
            xp[h, c, p] = xp[h, c, p] + rxp[h, p]
        x1[h].start()

    class Hop:
        def __init__(self, sem, axis, src, dst):
            self.sem, self.axis, self.src, self.dst = sem, axis, src, dst
            self.p = coord[axis]

        def start(self):
            self.a = []
            for i, sh in enumerate(SHIFTS):
                sem = (*self.sem, i)
                self.a.append(remote(self.src.at[add(self.p, sh)], self.dst.at[self.p],
                                     hop_s.at[sem], hop_r.at[sem], peer(self.axis, sh)))
            self.dst[self.p] = self.src[self.p]

        def finish(self):
            for cp in self.a:
                cp.wait_recv()

    if fast:
        rank = {a: rank_row(a) for a in ("x", "y")}
        slots = 2 * n * tb
        slotc = lax.broadcasted_iota(jnp.int32, (slots, 1), 0)
        lane = lax.broadcasted_iota(jnp.int32, (slots, vl), 1)
        for h in BOTH:
            a = axes[h][0]
            slot = (fr.c * n + fr.at[a]) * tb + rank[a]
            row = pick((slot == slotc) & fr.here & (rank[a] < tb), keyr)
            oh[pl.ds(h * slots, slots), :] = (row == lane).astype(BF16)

        def pack(h):
            eload[h].wait()

            @pl.loop(0, dh // cb)
            def _(j):
                cols = pl.ds(pl.multiple_of(j * cb, cb), cb)
                v = jnp.dot(oh[pl.ds(h * slots, slots), :], ebuf[h, :, cols], preferred_element_type=F32)
                xc[h, :, :, :, cols] = v.reshape(2, n, tb, cb).astype(BF16)

        def chosen(h, fixed, mine, slot_axis, rank_axis):
            other = "y" if slot_axis == "x" else "x"
            i = lax.broadcasted_iota(jnp.int32, (n * tb, 1), 0)
            q = i // tb
            yy, xx = (mine, q) if fixed == "y" else (q, mine)
            pos = ((i % tb) // tl) * t + ((yy * n + xx) * 2 + c) * tl + i % tl
            slot = fr.owner[slot_axis] * tb + rank[rank_axis]
            val = pick((posr == pos) & (fr.owner[other] == coord[other]) & (rank[rank_axis] < tb), slot)
            return (val == lax.broadcasted_iota(jnp.int32, (n * tb, n * tb), 1)).astype(BF16)

        hx = [Hop((0, h), axes[h][0], xc.at[h, c], rq.at[h]) for h in BOTH]
        he = [Hop((1, h), axes[h][1], cc_e.at[h], fx.at[h, c]) for h in BOTH]
        pack(0)
        xpair = [send_x(0)]
        start_d1(0)
        start_d1(1)
        pack(1)
        xpair.append(send_x(1))
        for h in BOTH:
            xpair[h].wait_recv()
            xc[h, c] = xc[h, c] + rxc[h]
            hx[h].start()
        for h in BOTH:
            d1[h].near(0)
        table()
        unpack = [chosen(h, axes[h][0], coord[axes[h][0]], axes[h][0], axes[h][0]) for h in BOTH]
        repack = [chosen(h, axes[h][1], coord[axes[h][1]], axes[h][1], axes[h][1]) for h in BOTH]
        for h in BOTH:
            d1[h].mid(0)
        for h in BOTH:
            hx[h].finish()
            for q in range(0, dh, dq):
                v = jnp.dot(unpack[h], rq[h, :, :, pl.ds(q, dq)].reshape(n * tb, dq), preferred_element_type=F32)
                tx[h, :, :, pl.ds(q, dq)] = v.reshape(n, tb, dq).astype(BF16)
            x2[h].start()
        for h in BOTH:
            d1[h].mid(1)
            d1[h].near(1)
        for h in BOTH:
            x2[h].mid()
    else:
        start_d1(0)
        start_d1(1)
        xpair = []
        for h in BOTH:
            eload[h].wait()
            emm(h)
            xpair.append(send_x(h))
        start_x1(0)
        for h in BOTH:
            d1[h].mid()
        start_x1(1)
        for h in BOTH:
            x1[h].mid()
        finish1(x1[0], tx, 0)
        x2[0].start()
        finish1(d1[0], t1, 0)
        d2[0].start()
        finish1(x1[1], tx, 1)
        x2[1].start()
        finish1(d1[1], t1, 1)
        d2[1].start()
        for h in BOTH:
            x2[h].mid()
        for h in BOTH:
            d2[h].mid()

    class Gather:
        def __init__(self, sem, axis, get, put=None):
            self.sem, self.axis, self.get, self.put = sem, axis, get, put
            self.p = coord[axis]
            self.sibs, self.a = [], []

        def send(self, msg, sgn, block, half):
            i = 0 if sgn > 0 else 1
            st, h, ph = self.sem
            ref = self.get(c, block, half)
            sem = (st * 2 + ph, h, msg, i)
            return remote(ref, ref, ag_s.at[sem], ag_r.at[sem], peer(self.axis, sgn))

        def have(self, s):
            if self.put is None:
                return
            st, h, _ = self.sem
            i = s % n
            ref = self.get(c, add(self.p, s), pl.ds(0, dh))
            self.sibs.append((s, remote(ref, ref, sib_s.at[st, h, i], sib_r.at[st, h, i], sib)))
            if st or not fast:
                self.out(c, s, 0)

        def out(self, cc, s, side):
            st, h, _ = self.sem
            block = add(self.p, s)
            cp = pltpu.make_async_copy(self.get(cc, block, pl.ds(0, dh)), self.put(cc, block),
                                       osem.at[st, h, side, s % n])
            cp.start()
            outs.append(cp)

        def open(self, part):
            self.a += [self.send(part * 2, sg, self.p, pl.ds(part * dq, dq)) for sg in WAYS]

        def start(self):
            self.open(0)
            self.open(1)
            self.have(0)

        def mid(self):
            self.b = []
            for cp in self.a:
                cp.wait_recv()
            for sg in WAYS:
                self.b.append(self.send(1, sg, add(self.p, -sg), pl.ds(0 if sg > 0 else dq, dq)))
            for sg in WAYS:
                self.have(-sg)

        def finish(self):
            for cp in self.b:
                cp.wait_recv()
            self.have(2)

        def drain(self, count):
            for s, cp in self.sibs[:count]:
                cp.wait_recv()
                if not fast:
                    self.out(1 - c, s, 1)
            self.sibs = self.sibs[count:]

    def gathers(st, g, out):
        ph1, ph2 = [], []
        c0, c1 = pl.ds(0, dh), pl.ds(dh, dh)
        ph1.append(Gather((st, 0, 0), "x", lambda cc, i, hf: g.at[0, cc, y, i, :, hf]))
        ph2.append(Gather((st, 0, 1), "y", lambda cc, i, hf: g.at[0, cc, i, :, :, hf],
                          lambda cc, i: out.at[cc, i, :, :, c0]))
        ph1.append(Gather((st, 1, 0), "y", lambda cc, i, hf: g.at[1, cc, i, x, :, hf]))
        ph2.append(Gather((st, 1, 1), "x", lambda cc, i, hf: g.at[1, cc, :, i, :, hf],
                          lambda cc, i: out.at[cc, :, i, :, c1]))
        return ph1, ph2

    n1, n2 = gathers(0, gn, nall_ref)
    e1, e2 = gathers(1, gd, dxall_ref)

    for h in BOTH:
        for hf, v in x2[h].finish():
            own[0, h, :, hf] = v.astype(F32)
    ss = jnp.zeros((tb, 1), F32)
    for h in BOTH:
        v = own[0, h]
        ss = ss + jnp.sum(v * v, axis=-1, keepdims=True)
    rs = lax.rsqrt(ss / d + EPS)
    for h in BOTH:
        gf = gall[:, h * dh:(h + 1) * dh]
        gn[h, c, y, x] = (own[0, h] * rs * gf).astype(BF16)
        n1[h].start()
    for h in BOTH:
        v = own[0, h]
        for m in range(k):
            x_ref[m, :, pl.ds(h * dh, dh)] = v[m * tl:(m + 1) * tl].astype(BF16)
    emit(1, x_ref, xout_ref)

    if fast:
        for h in BOTH:
            finish1(d1[h], t1, h)
            d2[h].start()
        for h in BOTH:
            n1[h].mid()
        for h in BOTH:
            d2[h].mid()
        for h in BOTH:
            n1[h].finish()
            n2[h].open(0)

    for h in BOTH:
        for hf, v in d2[h].finish():
            own[1, h, :, hf] = v
    dot = jnp.zeros((tb, 1), F32)
    for h in BOTH:
        gf = gall[:, h * dh:(h + 1) * dh]
        nh = own[0, h] * rs
        dot = dot + jnp.sum(nh * (gf * own[1, h]), axis=-1, keepdims=True)
    dot = dot / d
    for h in BOTH:
        gf = gall[:, h * dh:(h + 1) * dh]
        nh = own[0, h] * rs
        dxn = rs * (gf * own[1, h] - nh * dot)
        dr = jnp.concatenate([dres_ref[m, :, pl.ds(h * dh, dh)].astype(F32) for m in range(k)], axis=0)
        gd[h, c, y, x] = (dr + dxn).astype(BF16)
        e1[h].start()
    for h in BOTH:
        dgp[:, pl.ds(h * dh, dh)] = jnp.sum(own[1, h] * (own[0, h] * rs), axis=0, keepdims=True)
    if fast:
        for h in BOTH:
            n2[h].open(1)
            n2[h].have(0)
    dgpair = remote(dgp, dgs, dg_s.at[0], dg_r.at[0], sib)

    if not fast:
        for h in BOTH:
            n1[h].mid()
    for h in BOTH:
        e1[h].mid()

    def spread(buf, axis, base):
        return [remote(buf.at[coord[axis]], buf.at[coord[axis]], dg_s.at[base + i], dg_r.at[base + i],
                       peer(axis, s)) for i, s in enumerate((1, -1, 2))]

    def total(buf):
        v = buf[0]
        for i in range(1, n):
            v = v + buf[i]
        return v

    if fast:
        for h in BOTH:
            n2[h].mid()
    dgpair.wait_recv()
    dgx[x] = dgp[...] + dgs[...]
    sx = spread(dgx, "x", 1)
    if not fast:
        for h in BOTH:
            n1[h].finish()
            n2[h].start()
    for h in BOTH:
        e1[h].finish()
        if not fast:
            e2[h].start()
            continue
        for q in range(0, dh, dq):
            cols = pl.ds(q, dq)
            blk = gd[0, c, y, :, :, cols] if h == 0 else gd[1, c, :, x, :, cols]
            v = lax.dot_general(repack[h], blk.reshape(n * tb, dq), (((0,), (0,)), ((), ())),
                                preferred_element_type=F32)
            cc_e[h, :, :, cols] = v.reshape(n, tb, dq).astype(BF16)
        he[h].start()
    for cp in sx:
        cp.wait_recv()
    dgy[y] = total(dgx)
    sy = spread(dgy, "y", 4)
    if not fast:
        for h in BOTH:
            n2[h].mid()
    if not fast:
        for h in BOTH:
            e2[h].mid()

    def finish_n():
        for h in BOTH:
            n2[h].finish()
        for cp in sy:
            cp.wait_recv()
        dg_ref[...] = total(dgy).reshape(d)
        emit(2, dg_ref, dgout_ref)

    if fast:
        es = []
        for h in BOTH:
            he[h].finish()
            es.append(remote(fx.at[h, c], fx.at[h, c], sib_s.at[1, h, 0], sib_r.at[1, h, 0], sib))
            cp = pltpu.make_async_copy(fx.at[h, c], dxall_ref.at[0, c, :, :, pl.ds(h * dh, dh)], osem.at[1, h, 0])
            cp.start()
            outs.append(cp)
        finish_n()
        def whole(h, cc, i):
            cp = pltpu.make_async_copy(gn.at[h, cc], nall_ref.at[cc, :, :, :, pl.ds(h * dh, dh)], osem.at[0, h, i])
            cp.start()
            outs.append(cp)

        for h in BOTH:
            whole(h, c, 0)
        for h in BOTH:
            n2[h].drain(n)
        for h in BOTH:
            whole(h, 1 - c, 1)
        for h in BOTH:
            es[h].wait_recv()
            cp = pltpu.make_async_copy(fx.at[h, 1 - c], dxall_ref.at[0, 1 - c, :, :, pl.ds(h * dh, dh)],
                                       osem.at[1, h, 1])
            cp.start()
            outs.append(cp)
    else:
        finish_n()
        for h in BOTH:
            n2[h].drain(4)
        for h in BOTH:
            e2[h].drain(1)
        for h in BOTH:
            e2[h].finish()
        for i in (2, 1):
            for h in BOTH:
                e2[h].drain(i)
    for cp in sends:
        cp.wait_send()
    for cp in outs:
        cp.wait()


def load_kernel(dims, ids_ref, most_ref):
    k, tl, n = dims["k"], dims["tl"], dims["n"]
    t = ids_ref.shape[1]
    rows = dims["rt"] * 16
    ids = ids_ref[...]
    idt = jnp.transpose(jnp.concatenate([ids, jnp.zeros((8 - k, t), jnp.int32)], axis=0))
    keys = []
    for axis in BOTH:
        tok = lax.broadcasted_iota(jnp.int32, ids.shape, 1) // tl
        tokt = lax.broadcasted_iota(jnp.int32, (t, 1), 0) // tl
        at = [(v // 2 % n if axis else v // (2 * n)) * 2 + v % 2 for v in (tok, tokt)]
        row = at[0] * (n * n) + ids // rows
        row = jnp.concatenate([row[m:m + 1] for m in range(k)], axis=1)
        col = jnp.concatenate([at[1] * (n * n) + idt[:, m:m + 1] // rows for m in range(k)], axis=0)
        keys.append(jnp.max(jnp.sum((row == col).astype(F32), axis=1, keepdims=True)))
    most_ref[0] = jnp.maximum(*keys).astype(jnp.int32)


def tail_kernel(dims, tab_ref, n_ref, dx_ref, w_ref, du_ref, x_ref, dg_ref,
                u_ref, de_ref, dw_ref, xo_ref, dgo_ref, dxb, dxf, dup, uacc, dsem):
    k, tl, side = dims["k"], dims["tl"], dims["n"]
    tb = k * tl
    rt = dims["rt"]
    j = pl.program_id(0)

    nd = 2 * side * tb
    d = dxf.shape[1]
    dh = d // 2

    @pl.when(j == 0)
    def _():
        pltpu.make_async_copy(dx_ref.at[pl.ds(0, nd)], dxb.at[pl.ds(0, nd)], dsem.at[0]).start()

    @pl.when(j == 1)
    def _():
        few = pltpu.make_async_copy(dx_ref.at[pl.ds(0, nd)], dxb.at[pl.ds(0, nd)], dsem.at[0])
        few.wait()
        dxf[pl.ds(0, nd), :] = dxb[pl.ds(0, nd), :].astype(F32)

        @pl.when(tab_ref[4, 0] == 1)
        def _():
            rest = pl.ds(nd, dxf.shape[0] - nd)
            more = pltpu.make_async_copy(dx_ref.at[rest], dxb.at[rest], dsem.at[1])
            more.start()
            more.wait()
            dxf[rest, :] = dxb[rest, :].astype(F32)

    @pl.when(j > 0)
    def _():
        de_ref[...] = jnp.zeros_like(de_ref)

        @pl.loop(tab_ref[3, j - 1], tab_ref[3, j])
        def _(i):
            row = pl.ds(tab_ref[0, i] - (j - 1) * rt, 1)
            for h in BOTH:
                cols = pl.ds(h * dh, dh)
                de_ref[row, cols] = de_ref[row, cols] + dxf[pl.ds(tab_ref[1 + h, i], 1), cols]

    @pl.when(j == 0)
    def _():
        duf = [du_ref[m].astype(F32) for m in range(k)]
        for cc in BOTH:
            for b in range(side * side):
                r = b * 2 + cc
                blk = jnp.concatenate([v[r * tl:(r + 1) * tl] for v in duf], axis=0)
                dup[pl.ds((cc * side * side + b) * tb, tb), :] = blk.astype(BF16)
        uacc[...] = jnp.zeros_like(uacc)
        xo_ref[...] = x_ref[...]
        dgo_ref[...] = dg_ref[...]

    @pl.when(j < dims["nw"])
    def _():
        nv = n_ref[...]
        dw_ref[...] = lax.dot_general(nv, dup[...], (((0,), (0,)), ((), ())), preferred_element_type=F32)
        uacc[...] += jnp.dot(nv, w_ref[...], preferred_element_type=F32)

    @pl.when(j == pl.num_programs(0) - 1)
    def _():
        for m in range(k):
            parts = []
            for b in range(side * side):
                for cc in BOTH:
                    row = (cc * side * side + b) * tb + m * tl
                    parts.append(uacc[pl.ds(row, tl), :])
            u_ref[m] = jnp.concatenate(parts, axis=0).astype(BF16)


def solution(mesh):
    groups = mesh.shape["tp"]
    side = math.isqrt(groups // 2)

    def local(ids, emb, g, w, du, dres):
        k, t = ids.shape
        vl, d = emb.shape
        f = w.shape[1]
        tl = t // groups
        tb = k * tl
        n = side
        dh, dq = d // 2, d // 4
        cw = 256 if dh % 256 == 0 else 128
        rt = vl // 8
        wc = d // 7 if d % 896 == 0 else d // 4
        nw = d // wc
        dims = dict(k=k, tl=tl, d=d, n=n, cw=cw, rt=rt, nw=nw, cb=dq)
        hbm = pl.BlockSpec(memory_space=pl.ANY)
        vm = pl.BlockSpec(memory_space=pltpu.VMEM)
        gshape = (2, 2, n, n, tb, dh)
        oshape = (2, n, n, tb, d)
        comm = lambda cid, fast: pl.pallas_call(
            functools.partial(comm_kernel, dict(dims, fast=fast)),
            out_shape=[
                jax.ShapeDtypeStruct((k, tl, d), BF16),
                jax.ShapeDtypeStruct(oshape, BF16),
                jax.ShapeDtypeStruct(oshape, BF16),
                jax.ShapeDtypeStruct((d,), F32),
                jax.ShapeDtypeStruct((8, k * t), jnp.int32),
            ],
            in_specs=[vm, hbm, vm, vm, vm, vm],
            out_specs=[hbm] * 5,
            scratch_shapes=[
                VMEM((2, vl, dh), BF16), DMA((2,)),
                VMEM((k * t, vl), BF16),
                VMEM((2, 2, n, n * tb, dh), BF16), VMEM((2, n, n * tb, dh), BF16),
                VMEM((2, n, n * tb, dh), F32), VMEM((2, 3, 2, n * tb, dq), F32),
                VMEM((2, n, tb, dh), F32), VMEM((2, 3, 2, tb, dq), F32),
                VMEM((2, 2, n, n * tb, dh), BF16), VMEM((2, n, n * tb, dh), BF16),
                VMEM((2, 3, 2, n * tb, dq), BF16),
                VMEM((2, n, tb, dh), BF16), VMEM((2, 3, 2, tb, dq), BF16),
                VMEM((2, 2, tb, dh), F32), VMEM(gshape, BF16), VMEM(gshape, BF16),
                VMEM((1, d), F32), VMEM((1, d), F32), VMEM((n, 1, d), F32), VMEM((n, 1, d), F32),
                *[DMA((2, 2))] * 2,
                *[DMA((2, 11, 2) if fast else (2, 2, 2, 3, 2))] * 2,
                *[DMA((3 if fast else 4, 2, 3, 2))] * 2,
                *[DMA((2, 2, n))] * 2,
                *[DMA((7,))] * 2, DMA((2, 2, 2) if fast else (2, 2, 2, n)),
                VMEM((2, 2, n, tb, dh), BF16), VMEM((2, n, tb, dh), BF16), VMEM((2, n, tb, dh), BF16),
                VMEM((2, n, tb, dh), BF16), VMEM((2, 2, n, tb, dh), BF16),
                *[DMA((2, 2, 3))] * 2,
                VMEM((k, tl, d), BF16), VMEM((d,), F32), VMEM((8, k * t), jnp.int32), DMA((3,)),
            ],
            compiler_params=pltpu.CompilerParams(collective_id=cid, has_side_effects=True,
                                                 vmem_limit_bytes=62 * 1024 * 1024),
        )
        most = pl.pallas_call(
            functools.partial(load_kernel, dims),
            out_shape=jax.ShapeDtypeStruct((1,), jnp.int32),
            in_specs=[vm],
            out_specs=pl.BlockSpec(memory_space=pltpu.SMEM),
        )(ids)[0]
        xo, nall, dxall, dg, tab = lax.cond(most <= tb, comm(0, True), comm(1, False), ids, emb, g, w, du, dres)
        u, de, dw, xo, dg = pl.pallas_call(
            functools.partial(tail_kernel, dims),
            grid=(vl // rt + 1,),
            out_shape=[
                jax.ShapeDtypeStruct((k, t, f), BF16),
                jax.ShapeDtypeStruct((vl, d), F32),
                jax.ShapeDtypeStruct((d, f), F32),
                jax.ShapeDtypeStruct((k, tl, d), BF16),
                jax.ShapeDtypeStruct((d,), F32),
            ],
            in_specs=[
                pl.BlockSpec(memory_space=pltpu.SMEM),
                pl.BlockSpec((k * t, wc), lambda j: (0, jnp.minimum(j, nw - 1))),
                hbm,
                pl.BlockSpec((wc, f), lambda j: (jnp.minimum(j, nw - 1), 0)),
                pl.BlockSpec((k, t, f), lambda j: (0, 0, 0)),
                pl.BlockSpec((k, tl, d), lambda j: (0, 0, 0)),
                pl.BlockSpec((d,), lambda j: (0,)),
            ],
            out_specs=[
                pl.BlockSpec((k, t, f), lambda j: (0, 0, 0)),
                pl.BlockSpec((rt, d), lambda j: (jnp.maximum(j - 1, 0), 0)),
                pl.BlockSpec((wc, f), lambda j: (jnp.minimum(j, nw - 1), 0)),
                pl.BlockSpec((k, tl, d), lambda j: (0, 0, 0)),
                pl.BlockSpec((d,), lambda j: (0,)),
            ],
            scratch_shapes=[VMEM((k * t, d), BF16), VMEM((k * t, d), F32), VMEM((k * t, f), BF16),
                            VMEM((k * t, f), F32), DMA((2,))],
            compiler_params=pltpu.CompilerParams(vmem_limit_bytes=62 * 1024 * 1024),
        )(tab, nall.reshape(k * t, d), dxall.reshape(k * t, d), w, du, xo, dg)
        return u, xo, de, dw, dg

    return jax.shard_map(
        local,
        mesh=mesh,
        in_specs=(P("dp", None), P("tp", None), P(None), P(None, "tp"), P("dp", None, "tp"), P("dp", "tp", None)),
        out_specs=(P("dp", None, "tp"), P("dp", "tp", None), P(("dp", "tp"), None), P(None, ("dp", "tp")), P("dp")),
        check_vma=False,
    )
```

time: 93.4 us -> 82.8 us (0.89)
  Pallas kernels: 92.5 us -> 80.9 us
    pallas_call x2 -> x3, Pallas kernels: 92.5 us -> 80.9 us  [the longest x1 63.9 us: local(): lax.cond(most <= tb, comm(0, True), comm(1, False), ids, emb, g, w, du, d...]
where the time goes in v3:
time: 82.8 us; the launch traced here: 82.5 us
  Pallas kernels  80.9 us (98%)
  between operations  1.46 us (2%)
    pallas_call x1, Pallas kernels, local(): lax.cond(most <= tb, comm(0, True), comm(1, False), ids, emb, g, w, du, d...  63.9 us
    pallas_call x1, Pallas kernels, local(): pl.pallas_call(functools.partial(tail_kernel, dims), grid=(vl // rt + 1,)...  15 us
    pallas_call x1, Pallas kernels, local(): pl.pallas_call(functools.partial(load_kernel, dims), out_shape=jax.ShapeD...  1.98 us

profile of v3, /device:TPU:97, one launch (start us, length us, event | category | flops | bytes accessed | tf_op | source)
XLA Modules:
  0.0 82.5 jit_solution(14918062842900703649)
XLA Ops:
  0.6 2.0 %shard_map.101 = s32[1]{0:T(128)} custom-call(s32[2,256]{1,0:T(2,128)} %ids_ref.1), custom_call_target="tpu_custom_call" | custom-call | tf_op jit(solution)/shard_map/pallas_call | solution.py:731
  3.3 64.1 %conditional.1 = (bf16[2,8,3584]{2,1,0:T(8,128)(2,1)S(1)}, f32[3584]{0:T(1024)S(1)}, s32[8,512]{1,0:T(8,128)S(1)}, bf16[512,3584]{1,0:T(8,128)(2,1)}, bf16[512,3584]{1,0:T(8,128)(2,1)}) conditional(s32[]{:T(128)} %bitcast.4, (s32[2,256]{1,0:T(2,128)}, bf16[2048,3584]{1,0:T(8,128)(2,1)}, bf16[3584]{0:T(1024)(128)(2,1)}, bf16[3584,256]{1,0:T(8,128)(2,1)}, ...), branch_computations={%region_0.0_spmd, %region_1.0_spmd} | conditional | bytes 40 | solution.py:737
  3.5 63.9 %branch_1_fun.1 = (bf16[2,8,3584]{2,1,0:T(8,128)(2,1)S(1)}, bf16[2,4,4,16,3584]{4,3,2,1,0:T(8,128)(2,1)}, bf16[2,4,4,16,3584]{4,3,2,1,0:T(8,128)(2,1)}, f32[3584]{0:T(1024)S(1)}, s32[8,512]{1,0:T(8,128)S(1)}) custom-call(s32[2,256]{1,0:T(2,128)} %get-tuple-element.47.ids_ref, bf16[2048,3584]{1,0:T(8,128)(2,1)} %get-tuple-element.48.emb_ref, ...), custom_call_target="tpu_custom_call" | custom-call | tf_op jit(solution)/shard_map/cond/branch_1_fun/pallas_call | solution.py:737
  67.4 15.0 %shard_map.102 = (bf16[2,256,256]{2,1,0:T(8,128)(2,1)}, f32[2048,3584]{1,0:T(8,128)}, f32[3584,256]{1,0:T(8,128)}, bf16[2,8,3584]{2,1,0:T(8,128)(2,1)}, f32[3584]{0:T(1024)}) custom-call(s32[8,512]{1,0:T(8,128)S(1)} %get-tuple-element.73.tab_ref, bf16[512,3584]{1,0:T(8,128)(2,1)} %get-tuple-element.74.n_ref, bf16[512,3584]{1,0:T(8,128)(2,1)} %get-tuple-element.75.dx_ref, ...), custom_call_target="tpu_custom_call" | custom-call | tf_op jit(solution)/shard_map/pallas_call | solution.py:738

commit v4 on v3

--- a/solution.py
+++ b/solution.py
@@ -327,9 +327,9 @@
             x2[h].start()
         for h in BOTH:
             d1[h].mid(1)
+        for h in BOTH:
+            x2[h].mid()
             d1[h].near(1)
-        for h in BOTH:
-            x2[h].mid()
     else:
         start_d1(0)
         start_d1(1)
@@ -459,7 +459,6 @@
             d2[h].mid()
         for h in BOTH:
             n1[h].finish()
-            n2[h].open(0)
 
     for h in BOTH:
         for hf, v in d2[h].finish():
@@ -481,6 +480,7 @@
         dgp[:, pl.ds(h * dh, dh)] = jnp.sum(own[1, h] * (own[0, h] * rs), axis=0, keepdims=True)
     if fast:
         for h in BOTH:
+            n2[h].open(0)
             n2[h].open(1)
             n2[h].have(0)
     dgpair = remote(dgp, dgs, dg_s.at[0], dg_r.at[0], sib)

time: 82.8 us -> 82.1 us (level)
  no operation moved by 1% of the time
where the time goes in v4:
time: 82.1 us; the launch traced here: 81.9 us
  Pallas kernels  80.2 us (98%)
  between operations  1.46 us (2%)
    pallas_call x1, Pallas kernels, local(): lax.cond(most <= tb, comm(0, True), comm(1, False), ids, emb, g, w, du, d...  63.2 us
    pallas_call x1, Pallas kernels, local(): pl.pallas_call(functools.partial(tail_kernel, dims), grid=(vl // rt + 1,)...  15 us
    pallas_call x1, Pallas kernels, local(): pl.pallas_call(functools.partial(load_kernel, dims), out_shape=jax.ShapeD...  1.98 us

profile of v4, /device:TPU:97, one launch (start us, length us, event | category | flops | bytes accessed | tf_op | source)
XLA Modules:
  0.0 81.9 jit_solution(3089656218884598477)
XLA Ops:
  0.6 2.0 %shard_map.101 = s32[1]{0:T(128)} custom-call(s32[2,256]{1,0:T(2,128)} %ids_ref.1), custom_call_target="tpu_custom_call" | custom-call | tf_op jit(solution)/shard_map/pallas_call | solution.py:731
  3.3 63.4 %conditional.1 = (bf16[2,8,3584]{2,1,0:T(8,128)(2,1)S(1)}, f32[3584]{0:T(1024)S(1)}, s32[8,512]{1,0:T(8,128)S(1)}, bf16[512,3584]{1,0:T(8,128)(2,1)}, bf16[512,3584]{1,0:T(8,128)(2,1)}) conditional(s32[]{:T(128)} %bitcast.4, (s32[2,256]{1,0:T(2,128)}, bf16[2048,3584]{1,0:T(8,128)(2,1)}, bf16[3584]{0:T(1024)(128)(2,1)}, bf16[3584,256]{1,0:T(8,128)(2,1)}, ...), branch_computations={%region_0.0_spmd, %region_1.0_spmd} | conditional | bytes 40 | solution.py:737
  3.5 63.2 %branch_1_fun.1 = (bf16[2,8,3584]{2,1,0:T(8,128)(2,1)S(1)}, bf16[2,4,4,16,3584]{4,3,2,1,0:T(8,128)(2,1)}, bf16[2,4,4,16,3584]{4,3,2,1,0:T(8,128)(2,1)}, f32[3584]{0:T(1024)S(1)}, s32[8,512]{1,0:T(8,128)S(1)}) custom-call(s32[2,256]{1,0:T(2,128)} %get-tuple-element.47.ids_ref, bf16[2048,3584]{1,0:T(8,128)(2,1)} %get-tuple-element.48.emb_ref, ...), custom_call_target="tpu_custom_call" | custom-call | tf_op jit(solution)/shard_map/cond/branch_1_fun/pallas_call | solution.py:737
  66.7 15.0 %shard_map.102 = (bf16[2,256,256]{2,1,0:T(8,128)(2,1)}, f32[2048,3584]{1,0:T(8,128)}, f32[3584,256]{1,0:T(8,128)}, bf16[2,8,3584]{2,1,0:T(8,128)(2,1)}, f32[3584]{0:T(1024)}) custom-call(s32[8,512]{1,0:T(8,128)S(1)} %get-tuple-element.73.tab_ref, bf16[512,3584]{1,0:T(8,128)(2,1)} %get-tuple-element.74.n_ref, bf16[512,3584]{1,0:T(8,128)(2,1)} %get-tuple-element.75.dx_ref, ...), custom_call_target="tpu_custom_call" | custom-call | tf_op jit(solution)/shard_map/pallas_call | solution.py:738
